TPU v7x, 256 devices: a 4x2x16 block of a 4x16x16 slice. The times are simulated.
256 devices in a mesh: grp: 2 (over y), col: 32 (over z, core), blk: 4 (over x).
Axes of the slice: x: 4, y: 2, z: 16, core: 2. Of those that a mesh axis runs over, the one named last changes fastest.
The devices are a block of a 4x16x16 slice.
Arguments:
- boundary: bfloat16 [256, 192, 576], P(('grp', 'col'), 'blk'), parts along dimension 0, may hold values from -6 to 6
- row_tensor: bfloat16 [256, 6, 6, 6, 6], P(('grp', 'col')), parts along dimension 0, may hold values from -1.5 to 1.5
- left_proj: bfloat16 [256, 192, 576], P(('grp', 'col'), 'blk'), parts along dimension 0, may hold values from -0.75 to 0.75
- right_proj: bfloat16 [256, 192, 576], P(('grp', 'col'), 'blk'), parts along dimension 0, may hold values from -0.3125 to 0.3125
- leg_parity: int32 [256, 3, 6], P('grp'), parts along dimension 0, may hold values from 0 to 1
- bond_charges: int32 [256, 2], P('grp'), parts along dimension 0, may hold values from 32 to 96, as said below
Outputs:
- new_boundary: bfloat16 [256, 192, 576], P(('grp', 'col'), 'blk'), parts along dimension 0
There are 2 independent parts, one for each index of `grp`. A program takes and returns all parts, laid end to end along the dimension named above; each array names one. Nothing has to cross between parts.
Inputs may be any that keep to these rules, and one draw needn't show every extreme that they name: `bond_charges`: odd counts are 128 minus these, so neither block of a bond holds more than 96 live rows; some bond has an even count of 96 and some bond an odd count of 96. `leg_parity`: [c, 0] is the horizontal leg left of column c, [c, 1] the vertical leg between boundary and row, [c, 2] the outgoing vertical leg.
All inputs are finite; a program needn't handle non-finite values.
Results may differ from a plain program's by a relative error of at most 0.0057.
Values may be sent and summed in bfloat16 or wider, within the bound.
A program may use at most 64 MiB of HBM per device.

v0:
```python
import jax
import jax.numpy as jnp
from jax import lax
from jax.sharding import PartitionSpec as P

CHI = 128
BLOCK = 96
D = 6


def from_everyone(x, axis):
    length = lax.axis_size(axis)
    return lax.all_to_all(jnp.broadcast_to(x[None], (length, *x.shape)), axis, 0, 0, tiled=True)


def joined_along(pieces, dim):
    dims = list(pieces.shape[1:])
    dims[dim] *= pieces.shape[0]
    return jnp.moveaxis(pieces, 0, dim).reshape(dims)


def gathered_copies(x, axis, dim):
    pieces = from_everyone(x, axis)
    return joined_along(pieces, dim)


def passed_along(x, axis, by):
    length = lax.axis_size(axis)
    return lax.ppermute(x, axis, [(i, (i + by) % length) for i in range(length)])


def live_rows(counts, parity, position):
    limit = jnp.where(parity == 0, counts, CHI - counts)
    return position < limit


def per_device(boundary, row_tensor, left_proj, right_proj, leg_parity, bond_charges):
    col_dev, sub_rows, merged = boundary.shape
    start_col = lax.axis_index("col") * col_dev
    charges_here = lax.dynamic_slice_in_dim(bond_charges, start_col, col_dev, 0)
    charges_next = lax.dynamic_slice_in_dim(jnp.roll(bond_charges, -1, 0), start_col, col_dev, 0)
    legs_here = lax.dynamic_slice_in_dim(leg_parity, start_col, col_dev, 0)
    legs_next = lax.dynamic_slice_in_dim(jnp.roll(leg_parity, -1, 0), start_col, col_dev, 0)
    in_here = charges_here[:, 0]
    out_here = charges_here[:, 1]
    in_next = charges_next[:, 0]
    out_next = charges_next[:, 1]
    left_leg = legs_here[:, 0]
    up_leg = legs_here[:, 1]
    down_leg = legs_here[:, 2]
    right_leg = legs_next[:, 0]
    inside = lax.iota(jnp.int32, BLOCK)
    row_start = lax.axis_index("blk") * sub_rows
    local_index = row_start + lax.iota(jnp.int32, sub_rows)
    local_parity = local_index // BLOCK
    local_position = local_index % BLOCK
    left_sel = (local_parity[None, :, None] + left_leg[:, None, :]) % 2
    left_mask = live_rows(out_here[:, None], local_parity[None, :], local_position[None, :])[
        :, :, None, None
    ] & live_rows(in_here[:, None, None, None], left_sel[..., None], inside[None, None, None, :])
    left_m = left_proj.reshape(col_dev, sub_rows, D, BLOCK) * left_mask.astype(jnp.bfloat16)
    left_dense = jnp.concatenate(
        [
            left_m * (left_sel == 0).astype(jnp.bfloat16)[..., None],
            left_m * (left_sel == 1).astype(jnp.bfloat16)[..., None],
        ],
        axis=3,
    )
    piece = gathered_copies(boundary, "blk", 1)
    count_rows = piece.shape[1]
    row_index = lax.iota(jnp.int32, count_rows)
    row_parity = row_index // BLOCK
    row_position = row_index % BLOCK
    bound_sel = (row_parity[None, :, None] + up_leg[:, None, :]) % 2
    bound_mask = live_rows(in_here[:, None], row_parity[None, :], row_position[None, :])[
        :, :, None, None
    ] & live_rows(in_next[:, None, None, None], bound_sel[..., None], inside[None, None, None, :])
    piece_m = piece.reshape(col_dev, count_rows, D, BLOCK) * bound_mask.astype(jnp.bfloat16)
    absorbed = jnp.einsum(
        "cpla,caub->cplub", left_dense, piece_m, preferred_element_type=jnp.float32
    ).astype(jnp.bfloat16)
    row_keep = (
        left_leg[:, :, None, None, None]
        + up_leg[:, None, :, None, None]
        + down_leg[:, None, None, :, None]
        + right_leg[:, None, None, None, :]
    ) % 2 == 0
    row_sign = 1 - 2 * left_leg[:, :, None, None, None] * up_leg[:, None, :, None, None]
    row_m = row_tensor * jnp.where(row_keep, row_sign, 0).astype(jnp.bfloat16)
    mixed = jnp.einsum("cplub,cludr->cpdrb", absorbed, row_m, preferred_element_type=jnp.float32)
    block_par = (
        local_parity[None, :, None, None] + down_leg[:, None, :, None] + right_leg[:, None, None, :]
    ) % 2
    sign_flip = (1 - 2 * block_par * down_leg[:, None, :, None]).astype(jnp.float32)
    mixed = (mixed * sign_flip[..., None]).astype(jnp.bfloat16)
    mixed_dense = jnp.concatenate(
        [
            mixed * (block_par == 0).astype(jnp.bfloat16)[..., None],
            mixed * (block_par == 1).astype(jnp.bfloat16)[..., None],
        ],
        axis=4,
    )
    incoming = passed_along(right_proj[:1], "col", -1)
    right_next = jnp.concatenate([right_proj[1:], incoming], axis=0)
    piece = gathered_copies(right_next, "blk", 1)
    count_rows = piece.shape[1]
    row_index = lax.iota(jnp.int32, count_rows)
    row_parity = row_index // BLOCK
    row_position = row_index % BLOCK
    right_sel = (row_parity[None, :, None] + right_leg[:, None, :]) % 2
    right_mask = live_rows(in_next[:, None], row_parity[None, :], row_position[None, :])[
        :, :, None, None
    ] & live_rows(out_next[:, None, None, None], right_sel[..., None], inside[None, None, None, :])
    piece_m = piece.reshape(col_dev, count_rows, D, BLOCK) * right_mask.astype(jnp.bfloat16)
    result = jnp.einsum(
        "cpdrb,cbre->cpde", mixed_dense, piece_m, preferred_element_type=jnp.float32
    )
    return result.astype(jnp.bfloat16).reshape(col_dev, sub_rows, merged)


def solution(mesh):
    in_specs = (
        P(("grp", "col"), "blk", None),
        P(("grp", "col"), None, None, None, None),
        P(("grp", "col"), "blk", None),
        P(("grp", "col"), "blk", None),
        P("grp", None, None),
        P("grp", None),
    )
    out_specs = P(("grp", "col"), "blk", None)
    return jax.shard_map(
        per_device, mesh=mesh, in_specs=in_specs, out_specs=out_specs, check_vma=False
    )
```

profile of v0, /device:TPU:34, one launch (start us, length us, event | category | flops | bytes accessed | tf_op | source)
XLA Modules:
  0.0 72.2 jit_solution(1000798347300259663)
XLA Ops:
  0.0 0.0 copy-start.10
  0.0 0.0 copy-start.6
  0.0 2.0 %broadcast_in_dim.170 = bf16[4,4,48,576]{3,2,1,0:T(8,128)(2,1)} broadcast(bf16[4,48,576]{2,1,0:T(8,128)(2,1)} %param.6), dimensions={1,2,3} | broadcast | bytes 1105920 | tf_op jit(solution)/shard_map/broadcast_in_dim | solution.py:13
  2.1 22.9 %all-to-all-start = ((bf16[4,4,48,576]{3,2,1,0:T(8,128)(2,1)}), bf16[4,4,48,576]{3,2,1,0:T(8,128)(2,1)S(1)}, u32[]{:S(2)}, u32[]{:S(2)}) async-start(bf16[4,4,48,576]{3,2,1,0:T(8,128)(2,1)} %broadcast_in_dim.170), calls=%async_computation | async-start | bytes 1966080 | tf_op jit(solution)/shard_map/all_to_all | solution.py:13
  24.9 0.0 copy-done.2
  25.0 3.5 %collective-permute-start = (bf16[1,48,576]{2,1,0:T(8,128)(2,1)S(1)}, bf16[1,48,576]{2,1,0:T(8,128)(2,1)S(1)}, u32[]{:S(2)}, u32[]{:S(2)}) collective-permute-start(bf16[1,48,576]{2,1,0:T(8,128)(2,1)S(1)} %slice.62), channel_id=1, source_target_pairs={{0,124},{4,0},{8,4},{12,8},{16,12},{20,16},{24,20},{28,24},{32,28}... | collective-permute-start | bytes 165896 | tf_op jit(solution)/shard_map/ppermute | solution.py:29
  28.4 0.0 copy-done.10
  28.4 0.1 slice.57
  28.5 0.1 pad_add_fusion
  28.6 0.1 constant_dynamic-slice_fusion.2
  28.8 0.0 copy-done.9
  28.8 0.1 slice.51
  28.8 0.1 constant_dynamic-slice_fusion.1
  28.9 0.1 copy.39
  29.0 0.1 copy.35
  29.1 0.1 copy.33
  29.2 0.1 copy.37
  29.3 0.1 copy.34
  29.4 0.1 fusion.39
  29.5 0.0 copy-done.6
  29.5 0.0 slice-start
  29.5 0.3 reshape.405
  29.8 0.1 copy.40
  29.9 0.1 copy.36
  30.0 0.1 copy.38
  30.1 0.1 broadcast_select_fusion
  30.2 1.2 %compare_convert_fusion.1 = (bf16[4,48,6,6]{3,1,2,0:T(8,128)(2,1)}, bf16[4,48,6,6]{3,1,2,0:T(8,128)(2,1)}) fusion(s32[4,6]{1,0:T(4,128)S(1)} %bitcast.62, s32[4,48,6]{1,2,0:T(8,128)S(1)} %get-tuple-element.32), kind=kLoop, calls=%fused_computation.51 | loop fusion | flops 110592 | bytes 32352 | tf_op jit(solution)/shard_map/convert_element_type | solution.py:98
  31.4 1.2 %subtract_convert_fusion = f32[4,48,6,6]{3,1,2,0:T(8,128)} fusion(s32[4,6]{1,0:T(4,128)S(1)} %broadcast_multiply_fusion.4, s32[4,6]{1,0:T(4,128)S(1)} %bitcast.63, s32[4,48,6]{1,2,0:T(8,128)S(1)} %get-tuple-element.32), kind=kLoop, calls=%fused_computation.46 | loop fusion | flops 103680 | bytes 32448 | tf_op jit(solution)/shard_map/convert_element_type | solution.py:94
  32.6 0.1 select_compare_fusion.2
  32.7 1.3 %fusion.32 = (s32[4,192,6]{2,1,0:T(8,128)}, s32[4,192,6]{2,1,0:T(8,128)}) fusion(s32[4]{0:T(128)S(1)} %get-tuple-element.25, s32[4]{0:T(128)S(1)} %get-tuple-element.21, s32[4,6]{1,0:T(4,128)S(1)} %bitcast.64, s32[192]{0:T(256)S(1)} %get-tuple-element.33, s32[4]{0:T(128)S(1)} %get-tuple-element.26, s32[4]{0:T(128)S(1)} %get-tuple-element.22, ...), kind=kLoop, calls=%fused_computation.59 | loop fusion | flops 129024 | bytes 37888 | tf_op jit(solution)/shard_map/jit(_where)/select_n | solution.py:33
  34.0 1.4 %broadcast_multiply_fusion.3 = (bf16[4,48,6,96]{3,1,2,0:T(8,128)(2,1)}, bf16[4,48,6,96]{3,1,2,0:T(8,128)(2,1)}) fusion(bf16[4,48,6]{1,2,0:T(8,128)(2,1)S(1)} %get-tuple-element.16, bf16[4,48,6,96]{3,2,1,0:T(8,128)(2,1)S(1)} %reshape.405, s32[4,48,6]{1,2,0:T(8,128)S(1)} %get-tuple-element.31, pred[4,48]{1,0:T(4,128)(4,1)S(1)} %select_compare_fusion.2, ...), kind=kLoop, calls=%fused_computation.66 | loop fusion | flops 1105920 | bytes 672960 | tf_op jit(solution)/shard_map/mul | solution.py:64
  35.4 0.0 copy-done.7
  35.4 1.3 %fusion.36 = bf16[4,6,6,6,6,1]{4,0,3,2,1,5:T(4,128)(2,1)} fusion(bf16[4,6,6,6,6]{4,0,3,2,1:T(4,128)(2,1)S(1)} %copy-done.7, s32[4,6,6]{0,2,1:T(8,128)S(1)} %get-tuple-element.15, s32[4,6]{1,0:T(4,128)S(1)} %bitcast.65, s32[4,6,6,6]{0,3,2,1:T(8,128)S(1)} %broadcast_add_fusion), kind=kLoop, calls=%fused_computation.64 | loop fusion | flops 98496 | bytes 24864 | tf_op jit(solution)/shard_map/mul | solution.py:89
  36.7 0.1 select_compare_fusion
  36.8 0.0 collective-permute-done
  36.8 0.0 slice-done
  36.8 0.0 all-to-all-done
  36.9 1.1 %broadcast_in_dim.176 = bf16[4,4,48,576]{3,2,1,0:T(8,128)(2,1)} broadcast(bf16[4,48,576]{2,1,0:T(8,128)(2,1)S(1)} %pad_maximum_fusion.1), dimensions={1,2,3} | broadcast | bytes 1105920 | tf_op jit(solution)/shard_map/broadcast_in_dim | solution.py:13
  37.9 4.8 %all-to-all-start.1 = ((bf16[4,4,48,576]{3,2,1,0:T(8,128)(2,1)}), bf16[4,4,48,576]{3,2,1,0:T(8,128)(2,1)S(1)}, u32[]{:S(2)}, u32[]{:S(2)}) async-start(bf16[4,4,48,576]{3,2,1,0:T(8,128)(2,1)} %broadcast_in_dim.176), calls=%async_computation.1 | async-start | bytes 1966080 | tf_op jit(solution)/shard_map/all_to_all | solution.py:13
  42.7 0.1 copy.42
  42.8 1.2 %reshape_reshape.6 = bf16[4,192,6,96]{3,2,1,0:T(8,128)(2,1)S(1)} reshape(bf16[4,4,48,576]{3,2,1,0:T(8,128)(2,1)S(1)} %copy.42) | data formatting | bytes 1769472 | tf_op jit(solution)/shard_map/reshape;reshape | solution.py:78
  44.1 0.0 copy-start
  44.1 0.0 copy-start.1
  44.1 4.8 %fusion.12 = bf16[4,192,6,96,1]{3,2,1,0,4:T(8,128)(2,1)S(1)} fusion(bf16[4,192,6,96]{3,2,1,0:T(8,128)(2,1)S(1)} %reshape_reshape.6, s32[4,192,6]{2,1,0:T(8,128)} %get-tuple-element.24, pred[4,192]{1,0:T(4,128)(4,1)S(1)} %get-tuple-element.19), kind=kLoop, calls=%fused_computation.15 | loop fusion | flops 1327104 | bytes 1788672 | tf_op jit(solution)/shard_map/mul | solution.py:78
  48.9 0.0 copy-start.3
  48.9 0.0 copy-start.4
  48.9 0.0 copy-start.5
  48.9 0.0 copy-start.8
  48.9 0.0 copy-done
  48.9 0.0 copy-done.1
  49.0 0.7 convert_bitcast_fusion
  49.6 0.3 copy-done.3
  50.0 0.1 copy-done.4
  50.0 0.1 copy-done.5
  50.1 0.1 copy-done.8
  50.2 6.6 %broadcast_multiply_fusion.1 = (bf16[4,48,6,6,96]{4,3,1,2,0:T(8,128)(2,1)S(1)}, bf16[4,48,6,6,96]{4,3,1,2,0:T(8,128)(2,1)S(1)}) fusion(bf16[4,48,6,6]{3,1,2,0:T(8,128)(2,1)S(1)} %copy-done.4, bf16[4,48,6,6]{3,1,2,0:T(8,128)(2,1)S(1)} %copy-done.5, f32[4,48,6,6]{3,1,2,0:T(8,128)S(1)} %copy-done.3, ...), kind=kOutput, calls=%fused_computation.21 | convolution fusion | flops 50429952 | bytes 4046976 | tf_op jit(solution)/shard_map/cplub,cludr->cpdrb/dot_general | solution.py:90
  56.8 4.5 %pad_maximum_fusion = bf16[4,48,6,6,192]{4,3,1,2,0:T(8,128)(2,1)} fusion(bf16[4,48,6,6,96]{4,3,1,2,0:T(8,128)(2,1)S(1)} %get-tuple-element.6, bf16[4,48,6,6,96]{4,3,1,2,0:T(8,128)(2,1)S(1)} %get-tuple-element.5), kind=kLoop, calls=%fused_computation | loop fusion | flops 5308416 | bytes 5308416 | tf_op jit(solution)/shard_map/concatenate | solution.py:96
  61.3 0.0 all-to-all-done.1
  61.3 0.1 copy.46
  61.4 1.2 %reshape_reshape.7 = bf16[4,192,6,96]{3,2,1,0:T(8,128)(2,1)S(1)} reshape(bf16[4,4,48,576]{3,2,1,0:T(8,128)(2,1)S(1)} %copy.46) | data formatting | bytes 1769472 | tf_op jit(solution)/shard_map/reshape;reshape | solution.py:114
  62.6 4.7 %fusion.11 = bf16[4,192,6,96,1]{3,2,1,0,4:T(8,128)(2,1)S(1)} fusion(bf16[4,192,6,96]{3,2,1,0:T(8,128)(2,1)S(1)} %reshape_reshape.7, s32[4,192,6]{2,1,0:T(8,128)} %get-tuple-element.23, pred[4,192]{1,0:T(4,128)(4,1)S(1)} %get-tuple-element.18), kind=kLoop, calls=%fused_computation.14 | loop fusion | flops 1327104 | bytes 1788672 | tf_op jit(solution)/shard_map/mul | solution.py:114
  67.4 3.7 %fusion.16 = bf16[4,48,6,96]{3,1,2,0:T(8,128)(2,1)S(1)} fusion(bf16[4,48,6,6,192]{4,3,1,2,0:T(8,128)(2,1)} %pad_maximum_fusion, bf16[4,192,6,96,1]{3,2,1,0,4:T(8,128)(2,1)S(1)} %fusion.11), kind=kOutput, calls=%fused_computation.17 | convolution fusion | flops 254914560 | bytes 3760128 | tf_op jit(solution)/shard_map/cpdrb,cbre->cpde/dot_general | solution.py:115
  71.1 0.1 copy.49
  71.2 1.0 %reshape.406 = bf16[4,48,576]{2,1,0:T(8,128)(2,1)} reshape(bf16[4,48,6,96]{3,2,1,0:T(8,128)(2,1)S(1)} %copy.49) | data formatting | bytes 442368 | tf_op jit(solution)/shard_map/reshape | solution.py:118
  (17 shorter events, 0.1 us)
Async XLA Ops:
  0.0 24.9 %copy-start.2 = (bf16[4,48,576]{2,1,0:T(8,128)(2,1)S(1)}, bf16[4,48,576]{2,1,0:T(8,128)(2,1)}, u32[]{:S(2)}) copy-start(bf16[4,48,576]{2,1,0:T(8,128)(2,1)} %param.9) | copy-start | bytes 663556
  0.0 28.4 %copy-start.10 = (s32[128,2]{0,1:T(2,128)S(1)}, s32[128,2]{0,1:T(2,128)}, u32[]{:S(2)}) copy-start(s32[128,2]{0,1:T(2,128)} %param.11) | copy-start | bytes 3076
  0.0 28.8 %copy-start.9 = (s32[128,3,6]{0,2,1:T(8,128)S(1)}, s32[128,3,6]{0,2,1:T(8,128)}, u32[]{:S(2)}) copy-start(s32[128,3,6]{0,2,1:T(8,128)} %param.10) | copy-start | bytes 27652
  0.0 29.5 %copy-start.6 = (bf16[4,48,576]{2,1,0:T(8,128)(2,1)S(1)}, bf16[4,48,576]{2,1,0:T(8,128)(2,1)}, u32[]{:S(2)}) copy-start(bf16[4,48,576]{2,1,0:T(8,128)(2,1)} %param.8) | copy-start | bytes 663556
  2.1 34.8 %all-to-all-start = ((bf16[4,4,48,576]{3,2,1,0:T(8,128)(2,1)}), bf16[4,4,48,576]{3,2,1,0:T(8,128)(2,1)S(1)}, u32[]{:S(2)}, u32[]{:S(2)}) async-start(bf16[4,4,48,576]{3,2,1,0:T(8,128)(2,1)} %broadcast_in_dim.170), calls=%async_computation | async-start | bytes 1966080 | tf_op jit(solution)/shard_map/all_to_all | solution.py:13
  24.9 10.5 %copy-start.7 = (bf16[4,6,6,6,6]{4,0,3,2,1:T(4,128)(2,1)S(1)}, bf16[4,6,6,6,6]{4,0,3,2,1:T(4,128)(2,1)}, u32[]{:S(2)}) copy-start(bf16[4,6,6,6,6]{4,0,3,2,1:T(4,128)(2,1)} %param.7) | copy-start | bytes 31108
  25.0 11.8 %collective-permute-start = (bf16[1,48,576]{2,1,0:T(8,128)(2,1)S(1)}, bf16[1,48,576]{2,1,0:T(8,128)(2,1)S(1)}, u32[]{:S(2)}, u32[]{:S(2)}) collective-permute-start(bf16[1,48,576]{2,1,0:T(8,128)(2,1)S(1)} %slice.62), channel_id=1, source_target_pairs={{0,124},{4,0},{8,4},{12,8},{16,12},{20,16},{24,20},{28,24},{32,28}... | collective-permute-start | bytes 165896 | tf_op jit(solution)/shard_map/ppermute | solution.py:29
  29.5 7.3 %slice-start = ((bf16[4,48,576]{2,1,0:T(8,128)(2,1)}), bf16[3,48,576]{2,1,0:T(8,128)(2,1)S(1)}, s32[]{:S(2)}) async-start(bf16[4,48,576]{2,1,0:T(8,128)(2,1)} %param.9), calls=%async_computation.2 | async-start | bytes 368640 | tf_op jit(solution)/shard_map/slice | solution.py:104
  37.9 23.4 %all-to-all-start.1 = ((bf16[4,4,48,576]{3,2,1,0:T(8,128)(2,1)}), bf16[4,4,48,576]{3,2,1,0:T(8,128)(2,1)S(1)}, u32[]{:S(2)}, u32[]{:S(2)}) async-start(bf16[4,4,48,576]{3,2,1,0:T(8,128)(2,1)} %broadcast_in_dim.176), calls=%async_computation.1 | async-start | bytes 1966080 | tf_op jit(solution)/shard_map/all_to_all | solution.py:13
  44.1 4.9 %copy-start = (bf16[4,48,6,96]{3,1,2,0:T(8,128)(2,1)S(1)}, bf16[4,48,6,96]{3,1,2,0:T(8,128)(2,1)}, u32[]{:S(2)}) copy-start(bf16[4,48,6,96]{3,1,2,0:T(8,128)(2,1)} %get-tuple-element.7) | copy-start | bytes 663556
  44.1 4.9 %copy-start.1 = (bf16[4,48,6,96]{3,1,2,0:T(8,128)(2,1)S(1)}, bf16[4,48,6,96]{3,1,2,0:T(8,128)(2,1)}, u32[]{:S(2)}) copy-start(bf16[4,48,6,96]{3,1,2,0:T(8,128)(2,1)} %get-tuple-element.8) | copy-start | bytes 663556
  48.9 1.1 %copy-start.3 = (f32[4,48,6,6]{3,1,2,0:T(8,128)S(1)}, f32[4,48,6,6]{3,1,2,0:T(8,128)}, u32[]{:S(2)}) copy-start(f32[4,48,6,6]{3,1,2,0:T(8,128)} %subtract_convert_fusion) | copy-start | bytes 82948
  48.9 1.1 %copy-start.4 = (bf16[4,48,6,6]{3,1,2,0:T(8,128)(2,1)S(1)}, bf16[4,48,6,6]{3,1,2,0:T(8,128)(2,1)}, u32[]{:S(2)}) copy-start(bf16[4,48,6,6]{3,1,2,0:T(8,128)(2,1)} %get-tuple-element.9) | copy-start | bytes 41476
  48.9 1.2 %copy-start.5 = (bf16[4,48,6,6]{3,1,2,0:T(8,128)(2,1)S(1)}, bf16[4,48,6,6]{3,1,2,0:T(8,128)(2,1)}, u32[]{:S(2)}) copy-start(bf16[4,48,6,6]{3,1,2,0:T(8,128)(2,1)} %get-tuple-element.10) | copy-start | bytes 41476
  48.9 1.3 %copy-start.8 = (bf16[4,6,6,6,6,1]{4,0,3,2,1,5:T(4,128)(2,1)S(1)}, bf16[4,6,6,6,6,1]{4,0,3,2,1,5:T(4,128)(2,1)}, u32[]{:S(2)}) copy-start(bf16[4,6,6,6,6,1]{4,0,3,2,1,5:T(4,128)(2,1)} %fusion.36) | copy-start | bytes 31108
where the time goes:
time: 73.1 us; the launch traced here: 72.2 us
  starting transfers between devices  31.2 us (43%)
  other arithmetic  21.1 us (29%)
  matrix products  11 us (15%)
  local copies, waits for them, and re-layouts  8.69 us (12%)
    all_to_all x2, starting transfers between devices, from_everyone(): lax.all_to_all(jnp.broadcast_to(x[None], (length, *x.shape)), axis, 0, 0,...  27.7 us
    mul x2, other arithmetic, per_device(): piece.reshape(col_dev, count_rows, D, BLOCK)  9.55 us
    dot_general x1, matrix products, per_device(): jnp.einsum('cplub,cludr->cpdrb', absorbed, row_m, preferred_element_type=...  6.61 us
    concatenate x1, other arithmetic, per_device(): jnp.concatenate([mixed * (block_par == 0).astype(jnp.bfloat16)[..., None]...  4.49 us
    dot_general x1, matrix products, per_device(): jnp.einsum('cpdrb,cbre->cpde', mixed_dense, piece_m, preferred_element_ty...  3.73 us
    ppermute x1, starting transfers between devices, passed_along(): lax.ppermute(x, axis, [(i, (i + by) % length) for i in range(length)])  3.48 us
    broadcast_in_dim x2, local copies, waits for them, and re-layouts, from_everyone(): jnp.broadcast_to(x[None], (length, *x.shape))  3.12 us
    another operation x2, local copies, waits for them, and re-layouts, per_device(): piece.reshape(col_dev, count_rows, D, BLOCK)  2.45 us
  transfers between devices with their start and end apart: 3, of which 0 were waited for; matrix products, arithmetic and copies ran while one was open for 36% of the time, Pallas kernels for 0%

commit v1 on v0

v1 whole, which is shorter than its diff:
```python
import functools

import jax
import jax.numpy as jnp
from jax import lax
from jax.experimental import pallas as pl
from jax.experimental.pallas import tpu as pltpu
from jax.sharding import PartitionSpec as P

CHI = 128
BLOCK = 96
D = 6
LANES = 128
SUB = 16
PAIRS = D * D
WIDE = PAIRS * SUB

MESH = pl.DeviceIdType.MESH
F32 = jnp.float32
BF16 = jnp.bfloat16


def ones_where(condition):
    return jnp.where(condition, 1.0, 0.0).astype(F32)


def iota(shape, dim):
    return lax.broadcasted_iota(jnp.int32, shape, dim)


def by_group(scalars, index, width):
    out = jnp.full(index.shape, scalars[0], jnp.int32)
    for i in range(1, len(scalars)):
        out = jnp.where(index >= i * width, scalars[i], out)
    return out


def limit_of(count, parity):
    return jnp.where(parity == 0, count, CHI - count)


def kernel(axis_sizes, bound_ref, left_ref, right_ref, row_ref, leg_ref, bond_ref, out_ref,
           bound_all, left_all, right_all, bound_x, left_x, right_x, mix, mid, dense, answer,
           send_sem, recv_sem, local_sem):
    n_col, n_blk = axis_sizes
    col_dev, sub_rows, merged = bound_ref.shape
    me = lax.axis_index("blk")
    col = lax.axis_index("col")
    last = n_blk - 1
    col_before = lax.rem(col + n_col - 1, n_col)
    col_after = lax.rem(col + 1, n_col)
    cols = bond_ref.shape[1]
    here = col * col_dev + me
    after = lax.rem(here + 1, cols)

    barrier = pltpu.get_barrier_semaphore()
    for k in range(1, n_blk):
        pl.semaphore_signal(barrier, inc=1, device_id={"blk": lax.rem(me + k, n_blk)}, device_id_type=MESH)

    @pl.when(me == last)
    def _():
        for t in range(n_blk):
            pl.semaphore_signal(barrier, inc=1, device_id={"col": col_after, "blk": t}, device_id_type=MESH)

    def rows(t):
        return pl.ds(pl.multiple_of(t * sub_rows, SUB), sub_rows)

    own_bound = pltpu.make_async_copy(bound_ref.at[me], bound_all.at[rows(me)], local_sem.at[0])
    own_left = pltpu.make_async_copy(left_ref.at[me], left_all.at[rows(me)], local_sem.at[1])
    own_bound.start()
    own_left.start()
    own_right = pltpu.make_async_copy(right_ref.at[lax.rem(me + 1, col_dev)], right_all.at[rows(me)], local_sem.at[2])

    @pl.when(me != last)
    def _():
        own_right.start()

    pl.semaphore_wait(barrier, n_blk)

    def sent(kind, k):
        t = lax.rem(me + k, n_blk)
        if kind == 0:
            source, target, where = bound_ref.at[t], bound_all, {"blk": t}
        elif kind == 1:
            source, target, where = left_ref.at[t], left_all, {"blk": t}
        else:
            c = jnp.where(t == last, col_before, col)
            source, target, where = right_ref.at[lax.rem(t + 1, col_dev)], right_all, {"col": c, "blk": t}
        return pltpu.make_async_remote_copy(
            src_ref=source, dst_ref=target.at[rows(me)],
            send_sem=send_sem.at[kind, k], recv_sem=recv_sem.at[kind, me],
            device_id=where, device_id_type=MESH)

    def arrived(kind, k):
        t = lax.rem(me + k, n_blk)
        source = (bound_ref, left_ref, right_ref)[kind]
        target = (bound_all, left_all, right_all)[kind]
        return pltpu.make_async_remote_copy(
            src_ref=source.at[0], dst_ref=target.at[rows(t)],
            send_sem=send_sem.at[kind, k], recv_sem=recv_sem.at[kind, t],
            device_id={"blk": t}, device_id_type=MESH)

    far_first = [2, 1, 3] if n_blk == 4 else list(range(1, n_blk))
    for kind in range(3):
        for k in far_first:
            sent(kind, k).start()

    @pl.when(me == last)
    def _():
        sent(2, 0).start()

    p0 = [leg_ref[0, i, here] for i in range(D)]
    p1 = [leg_ref[1, i, here] for i in range(D)]
    p2 = [leg_ref[2, i, here] for i in range(D)]
    pr = [leg_ref[0, i, after] for i in range(D)]
    in_here, out_here = bond_ref[0, here], bond_ref[1, here]
    in_next, out_next = bond_ref[0, after], bond_ref[1, after]

    triples = D * D * D
    pick = ones_where(iota((triples, triples * col_dev), 1) == iota((triples, triples * col_dev), 0) * col_dev + me)
    entries = jnp.dot(pick.astype(BF16), row_ref[...], preferred_element_type=F32).astype(BF16)
    lane = iota((D, LANES), 1)
    spread = ones_where((lane - iota((D, LANES), 0)) % D == 0)
    entries = jnp.dot(entries, spread.astype(BF16), preferred_element_type=F32)
    row = iota((triples, LANES), 0)
    lane = iota((triples, LANES), 1)
    d_row = row % D
    d_lane = lane // D
    legs_l = by_group(p0, row, D * D)
    legs_u = by_group(p1, (row // D) % D, 1)
    legs_d = by_group(p2, d_row, 1)
    legs_r = by_group(pr, lane % D, 1)
    total = legs_l + legs_u + legs_d + legs_r
    keep = (d_row == d_lane) & (total % 2 == 0)
    sign = 1 - 2 * legs_l * legs_u
    group = iota((WIDE, triples), 0) // SUB
    member = iota((WIDE, triples), 1)
    repeat = ones_where((member >= group * D) & (member < group * D + D)).astype(BF16)
    pair = ones_where(iota((WIDE, LANES), 0) // SUB == iota((WIDE, LANES), 1)).astype(BF16)
    same = ones_where(iota((WIDE, WIDE), 0) % SUB == iota((WIDE, WIDE), 1) % SUB)
    for p in range(2):
        q = (p + legs_d + legs_r) % 2
        signed = jnp.where(keep, sign * (1 - 2 * q * legs_d), 0).astype(F32)
        picked = (entries * signed).astype(BF16)
        stretched = jnp.dot(repeat, picked, preferred_element_type=F32).astype(BF16)
        full = lax.dot_general(pair, stretched, (((1,), (1,)), ((), ())), preferred_element_type=F32)
        mix[p] = (full * same).astype(BF16)

    zeros = jnp.zeros((2 * LANES - 2 * BLOCK, D * LANES), BF16)
    gap = LANES - BLOCK
    for p in range(2):
        bound_x[p * LANES + BLOCK:(p + 1) * LANES, :] = zeros[:gap]
    for r in range(D):
        right_x[r * LANES + BLOCK:(r + 1) * LANES, :] = zeros[:gap, :2 * LANES]
    lane_pad = jnp.zeros((sub_rows, gap), BF16)

    def widened(value, i):
        return jnp.concatenate([value[:, i * BLOCK:(i + 1) * BLOCK], lane_pad], axis=1)

    own_bound.wait()
    for k in far_first:
        arrived(0, k).wait_recv()
    for t in range(n_blk):
        p, half = t // 2, t % 2
        live = ones_where(half * sub_rows + iota((sub_rows, LANES), 0) < limit_of(in_here, p)).astype(BF16)
        value = bound_all[t * sub_rows:(t + 1) * sub_rows, :]
        for u in range(D):
            bound_x[p * LANES + half * sub_rows:p * LANES + (half + 1) * sub_rows,
                    u * LANES:(u + 1) * LANES] = widened(value, u) * live

    own_left.wait()
    for k in far_first:
        arrived(1, k).wait_recv()

    def right_ready():
        for k in far_first:
            arrived(2, k).wait_recv()

        @pl.when(me == last)
        def _():
            arrived(2, 0).wait_recv()

        @pl.when(me != last)
        def _():
            own_right.wait()

        for half in range(2):
            even = right_all[half * sub_rows:(half + 1) * sub_rows, :]
            odd = right_all[BLOCK + half * sub_rows:BLOCK + (half + 1) * sub_rows, :]
            position = half * sub_rows + iota((sub_rows, LANES), 0)
            even_live = ones_where(position < limit_of(in_next, 0)).astype(BF16)
            odd_live = ones_where(position < limit_of(in_next, 1)).astype(BF16)
            for r in range(D):
                a = widened(even, r) * even_live
                b = widened(odd, r) * odd_live
                at = slice(r * LANES + half * sub_rows, r * LANES + (half + 1) * sub_rows)
                right_x[at, :LANES] = jnp.where(pr[r] == 0, a, b)
                right_x[at, LANES:] = jnp.where(pr[r] == 0, b, a)

    own_half = me // 2
    groups = BLOCK // SUB
    for step in range(2):
        p = (own_half + 1 + step) % 2
        for half in range(2):
            value = left_all[pl.ds(pl.multiple_of(p * BLOCK + half * sub_rows, SUB), sub_rows), :]
            for leg in range(D):
                wide = widened(value, leg)
                at = slice(leg * BLOCK + half * sub_rows, leg * BLOCK + (half + 1) * sub_rows)
                odd = ((p + p0[leg]) % 2).astype(F32)
                left_x[at, :LANES] = wide * (1.0 - odd).astype(BF16)
                left_x[at, LANES:] = wide * odd.astype(BF16)
        for n in range(D // 2):
            part = jnp.dot(left_x[...], bound_x[:, n * 2 * LANES:(n + 1) * 2 * LANES],
                           preferred_element_type=F32).astype(BF16)
            for leg in range(D):
                for v in range(2):
                    at = (leg * D + 2 * n + v) * SUB
                    for g in range(groups):
                        mid[at:at + SUB, g * LANES:(g + 1) * LANES] = part[
                            leg * BLOCK + g * SUB:leg * BLOCK + (g + 1) * SUB, v * LANES:(v + 1) * LANES]
        for n in range(groups // 2):
            part = jnp.dot(mix[p], mid[:, n * 2 * LANES:(n + 1) * 2 * LANES],
                           preferred_element_type=F32).astype(BF16)
            for d in range(D):
                for r in range(D):
                    at = (d * D + r) * SUB
                    for v in range(2):
                        g = 2 * n + v
                        dense[d * BLOCK + g * SUB:d * BLOCK + (g + 1) * SUB, r * LANES:(r + 1) * LANES] = part[
                            at:at + SUB, v * LANES:(v + 1) * LANES]
        if step == 0:
            right_ready()
        position = iota((BLOCK, LANES), 0)
        row_live = position < limit_of(out_here, p)
        result = jnp.dot(dense[...], right_x[...], preferred_element_type=F32)
        for d in range(D):
            s = (p + p2[d]) % 2
            block = result[d * BLOCK:(d + 1) * BLOCK, :]
            chosen = jnp.where(s == 0, block[:, :LANES], block[:, LANES:])
            alive = row_live & (iota((BLOCK, LANES), 1) < limit_of(out_next, s))
            chosen = jnp.where(alive, chosen, 0.0).astype(BF16)[:, :BLOCK]
            for half in range(2):
                answer[2 * p + half, :, d * BLOCK:(d + 1) * BLOCK] = chosen[half * sub_rows:(half + 1) * sub_rows]
        for half in range(2):
            t = 2 * p + half

            @pl.when(t != me)
            def _():
                pltpu.make_async_remote_copy(
                    src_ref=answer.at[t], dst_ref=out_ref.at[me],
                    send_sem=send_sem.at[3, t], recv_sem=recv_sem.at[3, me],
                    device_id={"blk": t}, device_id_type=MESH).start()

            @pl.when(t == me)
            def _():
                pltpu.make_async_copy(answer.at[me], out_ref.at[me], local_sem.at[3]).start()

    pltpu.make_async_copy(answer.at[me], out_ref.at[me], local_sem.at[3]).wait()
    for k in far_first:
        t = lax.rem(me + k, n_blk)
        done = pltpu.make_async_remote_copy(
            src_ref=answer.at[t], dst_ref=out_ref.at[t],
            send_sem=send_sem.at[3, t], recv_sem=recv_sem.at[3, t],
            device_id={"blk": t}, device_id_type=MESH)
        done.wait_recv()
        done.wait_send()
        for kind in range(3):
            sent(kind, k).wait_send()

    @pl.when(me == last)
    def _():
        sent(2, 0).wait_send()


def per_device(axis_sizes, boundary, row_tensor, left_proj, right_proj, leg_parity, bond_charges):
    col_dev, sub_rows, merged = boundary.shape
    n_blk = axis_sizes[1]
    padded = n_blk * sub_rows
    rows = row_tensor.transpose(1, 2, 3, 0, 4).reshape(D * D * D * col_dev, D)
    anywhere = pl.BlockSpec(memory_space=pl.ANY)
    smem = pl.BlockSpec(memory_space=pltpu.SMEM)
    vmem = pl.BlockSpec(memory_space=pltpu.VMEM)
    return pl.pallas_call(
        functools.partial(kernel, axis_sizes),
        out_shape=jax.ShapeDtypeStruct(boundary.shape, BF16),
        in_specs=[anywhere, anywhere, anywhere, vmem, smem, smem],
        out_specs=vmem,
        scratch_shapes=[
            pltpu.VMEM((padded, merged), BF16),
            pltpu.VMEM((padded, merged), BF16),
            pltpu.VMEM((padded, merged), BF16),
            pltpu.VMEM((2 * LANES, D * LANES), BF16),
            pltpu.VMEM((D * BLOCK, 2 * LANES), BF16),
            pltpu.VMEM((D * LANES, 2 * LANES), BF16),
            pltpu.VMEM((2, WIDE, WIDE), BF16),
            pltpu.VMEM((WIDE, D * LANES), BF16),
            pltpu.VMEM((D * BLOCK, D * LANES), BF16),
            pltpu.VMEM((n_blk, sub_rows, merged), BF16),
            pltpu.SemaphoreType.DMA((4, n_blk)),
            pltpu.SemaphoreType.DMA((4, n_blk)),
            pltpu.SemaphoreType.DMA((4,)),
        ],
        compiler_params=pltpu.CompilerParams(collective_id=0, has_side_effects=True),
    )(boundary, left_proj, right_proj, rows, leg_parity.transpose(1, 2, 0), bond_charges.transpose(1, 0))


def solution(mesh):
    axis_sizes = (mesh.shape["col"], mesh.shape["blk"])
    in_specs = (
        P(("grp", "col"), "blk", None),
        P(("grp", "col"), None, None, None, None),
        P(("grp", "col"), "blk", None),
        P(("grp", "col"), "blk", None),
        P("grp", None, None),
        P("grp", None),
    )
    out_specs = P(("grp", "col"), "blk", None)
    return jax.shard_map(
        functools.partial(per_device, axis_sizes), mesh=mesh, in_specs=in_specs, out_specs=out_specs, check_vma=False
    )
```

time: 73.1 us -> 41.3 us (0.56)
  Pallas kernels: 0 us -> 38.8 us
  starting transfers between devices: 31.2 us -> 0 us
  other arithmetic: 21.1 us -> 0 us
  matrix products: 11 us -> 0 us
  local copies, waits for them, and re-layouts: 8.69 us -> 1.66 us
    pallas_call x0 -> x1, Pallas kernels: none -> 38.8 us  [per_device(): pl.pallas_call(functools.partial(kernel, axis_sizes), out_shape=jax.Shape...]
    all_to_all x2 -> x0, starting transfers between devices: 27.7 us -> none  [from_everyone(): lax.all_to_all(jnp.broadcast_to(x[None], (length, *x.shape)), axis, 0, 0,...]
    mul x6 -> x0, other arithmetic: 12.2 us -> none  [the longest x2 9.55 us: per_device(): piece.reshape(col_dev, count_rows, D, BLOCK)]
    dot_general x3 -> x0, matrix products: 11 us -> none  [the longest x1 6.61 us: per_device(): jnp.einsum('cplub,cludr->cpdrb', absorbed, row_m, preferred_element_type=...]
    concatenate x3 -> x0, other arithmetic: 4.6 us -> none  [the longest x1 4.49 us: per_device(): jnp.concatenate([mixed * (block_par == 0).astype(jnp.bfloat16)[..., None]...]
    ppermute x1 -> x0, starting transfers between devices: 3.48 us -> none  [passed_along(): lax.ppermute(x, axis, [(i, (i + by) % length) for i in range(length)])]
    broadcast_in_dim x2 -> x0, local copies, waits for them, and re-layouts: 3.12 us -> none  [from_everyone(): jnp.broadcast_to(x[None], (length, *x.shape))]
    convert_element_type x3 -> x0, other arithmetic: 2.52 us -> none  [the longest x1 1.24 us: per_device(): (block_par == 0).astype(jnp.bfloat16)[..., None]]
  transfers between devices with their start and end apart: 3 -> 0, of which waited for: 0 -> 0; matrix products, arithmetic and copies ran while one was open for 36% -> 0% of each run, Pallas kernels for 0% -> 0%
where the time goes in v1:
time: 41.3 us; the launch traced here: 40.5 us
  Pallas kernels  38.8 us (94%)
  local copies, waits for them, and re-layouts  1.66 us (4%)
    pallas_call x1, Pallas kernels, per_device(): pl.pallas_call(functools.partial(kernel, axis_sizes), out_shape=jax.Shape...  38.8 us
    unnamed x1, local copies, waits for them, and re-layouts  1.66 us

profile of v1, /device:TPU:34, one launch (start us, length us, event | category | flops | bytes accessed | tf_op | source)
XLA Modules:
  0.0 40.5 jit_solution(15110702724779988170)
XLA Ops:
  0.0 38.8 %shard_map.64 = bf16[4,48,576]{2,1,0:T(8,128)(2,1)} custom-call(bf16[4,48,576]{2,1,0:T(8,128)(2,1)} %bound_ref.1, bf16[4,48,576]{2,1,0:T(8,128)(2,1)} %left_ref.1, bf16[4,48,576]{2,1,0:T(8,128)(2,1)} %right_ref.1, bf16[864,6]{1,0:T(8,128)(2,1)} %bitcast.5, s32[3,6,128]{2,1,0:T(8,128)} %bitcast.6, s32[2,128]{1,0:T(2,128)} %bitcast.7), custom_call_target="tpu_custom_call" | custom-call | tf_op jit(solution)/shard_map/pallas_call | solution.py:283
  38.8 1.7 %copy.8 = bf16[4,48,576]{2,1,0:T(8,128)(2,1)} copy(bf16[4,48,576]{2,1,0:T(8,128)(2,1)} %shard_map.64) | data formatting | bytes 442368

commit v2 on v1

v2 whole, which is shorter than its diff:
```python
import functools

import jax
import jax.numpy as jnp
from jax import lax
from jax.experimental import pallas as pl
from jax.experimental.pallas import tpu as pltpu
from jax.sharding import PartitionSpec as P

CHI = 128
BLOCK = 96
D = 6
LANES = 128
SUB = 16
PAIRS = D * D
WIDE = PAIRS * SUB
VMEM_BYTES = 32 * 1024 * 1024

MESH = pl.DeviceIdType.MESH
F32 = jnp.float32
BF16 = jnp.bfloat16


def ones_where(condition):
    return jnp.where(condition, 1.0, 0.0).astype(F32)


def iota(shape, dim):
    return lax.broadcasted_iota(jnp.int32, shape, dim)


def by_group(scalars, index, width):
    out = jnp.full(index.shape, scalars[0], jnp.int32)
    for i in range(1, len(scalars)):
        out = jnp.where(index >= i * width, scalars[i], out)
    return out


def limit_of(count, parity):
    return jnp.where(parity == 0, count, CHI - count)


def kernel(axis_sizes, bound_ref, left_ref, right_ref, row_ref, leg_ref, bond_ref, out_ref,
           bound_all, left_all, left_shared, right_all, bound_x, left_x, right_x, mix, mid, dense, answer,
           send_sem, recv_sem, local_sem, ready_sem):
    n_col, n_blk = axis_sizes
    col_dev, sub_rows, merged = bound_ref.shape
    me = lax.axis_index("blk")
    col = lax.axis_index("col")
    last = n_blk - 1
    col_before = lax.rem(col + n_col - 1, n_col)
    col_after = lax.rem(col + 1, n_col)
    cols = bond_ref.shape[1]
    worker = me != 0

    barrier = pltpu.get_barrier_semaphore()
    pl.semaphore_signal(barrier, inc=1, device_id={"col": col_before, "blk": last}, device_id_type=MESH)

    @pl.when(worker)
    def _():
        for t in range(n_blk):
            @pl.when(me != t)
            def _():
                pl.semaphore_signal(barrier, inc=1, device_id={"blk": t}, device_id_type=MESH)

    def rows(t):
        return pl.ds(pl.multiple_of(t * sub_rows, SUB), sub_rows)

    targets = [bound_all.at[1], left_all, right_all.at[1], bound_all.at[0], right_all.at[0]]

    def source(kind, t):
        return (bound_ref.at[t], left_ref.at[t], right_ref.at[lax.rem(t + 1, col_dev)], bound_ref.at[0], right_ref.at[1])[kind]

    def own(kind):
        return pltpu.make_async_copy(source(kind, me), targets[kind].at[rows(me)], local_sem.at[kind])

    own(3).start()
    own(4).start()
    own_shared = pltpu.make_async_copy(left_ref.at[0], left_shared, local_sem.at[5])
    own_shared.start()

    @pl.when(worker)
    def _():
        own(0).start()
        own(1).start()

        @pl.when(me != last)
        def _():
            own(2).start()

    pl.semaphore_wait(barrier, jnp.where(me == 0, n_blk - 1, jnp.where(me == last, 2 * n_blk - 2, n_blk - 2)))

    def sent(kind, t):
        return pltpu.make_async_remote_copy(
            src_ref=source(kind, t), dst_ref=targets[kind].at[rows(me)],
            send_sem=send_sem.at[kind, t], recv_sem=recv_sem.at[kind, me],
            device_id={"blk": t}, device_id_type=MESH)

    def arrived(kind, t):
        return pltpu.make_async_remote_copy(
            src_ref=source(kind, 0), dst_ref=targets[kind].at[rows(t)],
            send_sem=send_sem.at[kind, t], recv_sem=recv_sem.at[kind, t],
            device_id={"blk": t}, device_id_type=MESH)

    beyond = pltpu.make_async_remote_copy(
        src_ref=right_ref.at[0], dst_ref=right_all.at[1, rows(me)],
        send_sem=send_sem.at[6, 0], recv_sem=recv_sem.at[2, me],
        device_id={"col": col_before, "blk": last}, device_id_type=MESH)

    @pl.when(me == 0)
    def _():
        for t in range(1, n_blk):
            pl.semaphore_signal(ready_sem.at[0], inc=1, device_id={"blk": t}, device_id_type=MESH)

    @pl.when(me == last)
    def _():
        for t in range(n_blk):
            pl.semaphore_signal(ready_sem.at[1], inc=1, device_id={"col": col_after, "blk": t}, device_id_type=MESH)

    kinds_to = {t: ([0, 2, 3, 4, 1] if t != last else [0, 3, 4, 1]) for t in range(1, n_blk)}
    for place in range(5):
        for t in (2, 1, 3):
            if place < len(kinds_to[t]):
                @pl.when(me != t)
                def _():
                    sent(kinds_to[t][place], t).start()

    triples = D * D * D
    group = iota((WIDE, triples), 0) // SUB
    member = iota((WIDE, triples), 1)
    repeat = ones_where((member >= group * D) & (member < group * D + D)).astype(BF16)
    pair = ones_where(iota((WIDE, LANES), 0) // SUB == iota((WIDE, LANES), 1)).astype(BF16)
    same = ones_where(iota((WIDE, WIDE), 0) % SUB == iota((WIDE, WIDE), 1) % SUB)
    spread = ones_where((iota((D, LANES), 1) - iota((D, LANES), 0)) % D == 0).astype(BF16)
    row = iota((triples, LANES), 0)
    lane = iota((triples, LANES), 1)
    d_row = row % D
    from_row = iota((triples, triples * col_dev), 0) * col_dev
    from_lane = iota((triples, triples * col_dev), 1)

    def legs_of(place):
        here = col * col_dev + place
        after = lax.rem(here + 1, cols)
        legs = [[leg_ref[i, j, here] for j in range(D)] for i in range(3)] + [[leg_ref[0, j, after] for j in range(D)]]
        return legs, (bond_ref[0, here], bond_ref[1, here], bond_ref[0, after], bond_ref[1, after])

    def build(place, legs, outputs):
        p0, p1, p2, pr = legs
        pick = ones_where(from_lane == from_row + place).astype(BF16)
        entries = jnp.dot(pick, row_ref[...], preferred_element_type=F32).astype(BF16)
        entries = jnp.dot(entries, spread, preferred_element_type=F32)
        legs_l = by_group(p0, row, D * D)
        legs_u = by_group(p1, (row // D) % D, 1)
        legs_d = by_group(p2, d_row, 1)
        legs_r = by_group(pr, lane % D, 1)
        keep = (d_row == lane // D) & ((legs_l + legs_u + legs_d + legs_r) % 2 == 0)
        sign = 1 - 2 * legs_l * legs_u
        for p, at in outputs:
            q = (p + legs_d + legs_r) % 2
            signed = jnp.where(keep, sign * (1 - 2 * q * legs_d), 0).astype(F32)
            stretched = jnp.dot(repeat, (entries * signed).astype(BF16), preferred_element_type=F32).astype(BF16)
            full = lax.dot_general(pair, stretched, (((1,), (1,)), ((), ())), preferred_element_type=F32)
            mix[at] = (full * same).astype(BF16)

    legs_shared, bonds_shared = legs_of(0)
    legs_mine, bonds_mine = legs_of(me)
    build(0, legs_shared, [(me // 2, 0)])

    @pl.when(worker)
    def _():
        build(me, legs_mine, [(0, 1), (1, 2)])

    gap = LANES - BLOCK
    lane_pad = jnp.zeros((sub_rows, gap), BF16)
    for slot in range(2):
        for p in range(2):
            bound_x[slot, p * LANES + BLOCK:(p + 1) * LANES, :] = jnp.zeros((gap, D * LANES), BF16)
        for r in range(D):
            right_x[slot, r * LANES + BLOCK:(r + 1) * LANES, :] = jnp.zeros((gap, 2 * LANES), BF16)

    @pl.when(worker)
    def _():
        pl.semaphore_wait(ready_sem.at[0], 1)
        sent(3, 0).start()
        sent(4, 0).start()

    def widened(value, i):
        return jnp.concatenate([value[:, i * BLOCK:(i + 1) * BLOCK], lane_pad], axis=1)

    def all_here(kind):
        for t in reversed(range(n_blk)):
            @pl.when(me != t)
            def _():
                arrived(kind, t).wait_recv()

            @pl.when(me == t)
            def _():
                if kind == 2 and t == last:
                    arrived(kind, t).wait_recv()
                else:
                    own(kind).wait()

    def boundary_ready(slot, bonds):
        all_here(0 if slot else 3)
        for t in range(n_blk):
            p, half = t // 2, t % 2
            live = ones_where(half * sub_rows + iota((sub_rows, LANES), 0) < limit_of(bonds[0], p)).astype(BF16)
            value = bound_all[slot, t * sub_rows:(t + 1) * sub_rows, :]
            at = p * LANES + half * sub_rows
            for u in range(D):
                bound_x[slot, at:at + sub_rows, u * LANES:(u + 1) * LANES] = widened(value, u) * live

    def right_ready(slot, legs, bonds):
        all_here(2 if slot else 4)
        pr = legs[3]
        for half in range(2):
            even = right_all[slot, half * sub_rows:(half + 1) * sub_rows, :]
            odd = right_all[slot, BLOCK + half * sub_rows:BLOCK + (half + 1) * sub_rows, :]
            position = half * sub_rows + iota((sub_rows, LANES), 0)
            even_live = ones_where(position < limit_of(bonds[2], 0)).astype(BF16)
            odd_live = ones_where(position < limit_of(bonds[2], 1)).astype(BF16)
            for r in range(D):
                a = widened(even, r) * even_live
                b = widened(odd, r) * odd_live
                at = slice(r * LANES + half * sub_rows, r * LANES + (half + 1) * sub_rows)
                right_x[slot, at, :LANES] = jnp.where(pr[r] == 0, a, b)
                right_x[slot, at, LANES:] = jnp.where(pr[r] == 0, b, a)

    groups = sub_rows // SUB

    def mixed_rows(slot, t, legs, value, buf):
        p = t // 2
        for leg in range(D):
            wide = widened(value, leg)
            odd = ((p + legs[0][leg]) % 2).astype(F32)
            left_x[buf, leg * sub_rows:(leg + 1) * sub_rows, :LANES] = wide * (1.0 - odd).astype(BF16)
            left_x[buf, leg * sub_rows:(leg + 1) * sub_rows, LANES:] = wide * odd.astype(BF16)
        for n in range(D // 2):
            part = jnp.dot(left_x[buf], bound_x[slot, :, n * 2 * LANES:(n + 1) * 2 * LANES],
                           preferred_element_type=F32).astype(BF16)
            for leg in range(D):
                for v in range(2):
                    at = (leg * D + 2 * n + v) * SUB
                    for g in range(groups):
                        mid[buf, at:at + SUB, g * LANES:(g + 1) * LANES] = part[
                            leg * sub_rows + g * SUB:leg * sub_rows + (g + 1) * SUB, v * LANES:(v + 1) * LANES]
        which = 0 if slot == 0 else 1 + p
        for lo in range(0, groups, 2):
            hi = min(lo + 2, groups)
            part = jnp.dot(mix[which], mid[buf, :, lo * LANES:hi * LANES], preferred_element_type=F32).astype(BF16)
            for d in range(D):
                for r in range(D):
                    at = (d * D + r) * SUB
                    for g in range(lo, hi):
                        dense[buf, d * sub_rows + g * SUB:d * sub_rows + (g + 1) * SUB, r * LANES:(r + 1) * LANES] = part[
                            at:at + SUB, (g - lo) * LANES:(g - lo + 1) * LANES]

    def new_rows(slot, t, legs, bonds, buf, target):
        p = t // 2
        position = (t % 2) * sub_rows + iota((sub_rows, LANES), 0)
        row_live = position < limit_of(bonds[1], p)
        result = jnp.dot(dense[buf], right_x[slot], preferred_element_type=F32)
        for d in range(D):
            s = (p + legs[2][d]) % 2
            block = result[d * sub_rows:(d + 1) * sub_rows, :]
            chosen = jnp.where(s == 0, block[:, :LANES], block[:, LANES:])
            alive = row_live & (iota((sub_rows, LANES), 1) < limit_of(bonds[3], s))
            target[:, d * BLOCK:(d + 1) * BLOCK] = jnp.where(alive, chosen, 0.0).astype(BF16)[:, :BLOCK]

    def returned(t):
        return pltpu.make_async_remote_copy(
            src_ref=answer.at[t], dst_ref=out_ref.at[me],
            send_sem=send_sem.at[5, t], recv_sem=recv_sem.at[5, me],
            device_id={"blk": t}, device_id_type=MESH)

    second = 1 + lax.rem(me, last)
    third = 1 + lax.rem(second, last)

    @pl.when(worker)
    def _():
        all_here(1)
        boundary_ready(1, bonds_mine)
        mixed_rows(1, second, legs_mine, left_all[rows(second), :], 0)

    pl.semaphore_wait(ready_sem.at[1], 1)
    beyond.start()

    @pl.when(worker)
    def _():
        right_ready(1, legs_mine, bonds_mine)
        new_rows(1, second, legs_mine, bonds_mine, 0, answer.at[second])
        returned(second).start()
        mixed_rows(1, third, legs_mine, left_all[rows(third), :], 1)
        new_rows(1, third, legs_mine, bonds_mine, 1, answer.at[third])
        returned(third).start()

    boundary_ready(0, bonds_shared)
    own_shared.wait()
    mixed_rows(0, me, legs_shared, left_shared[...], 0)
    right_ready(0, legs_shared, bonds_shared)
    new_rows(0, me, legs_shared, bonds_shared, 0, out_ref.at[0])

    @pl.when(worker)
    def _():
        mixed_rows(1, 0, legs_mine, left_all[rows(0), :], 1)
        new_rows(1, 0, legs_mine, bonds_mine, 1, answer.at[0])
        returned(0).start()
        mixed_rows(1, me, legs_mine, left_all[rows(me), :], 0)
        new_rows(1, me, legs_mine, bonds_mine, 0, out_ref.at[me])

    for t in range(1, n_blk):
        @pl.when(me != t)
        def _():
            pltpu.make_async_remote_copy(
                src_ref=answer.at[t], dst_ref=out_ref.at[t],
                send_sem=send_sem.at[5, t], recv_sem=recv_sem.at[5, t],
                device_id={"blk": t}, device_id_type=MESH).wait_recv()
            for kind in kinds_to[t]:
                sent(kind, t).wait_send()

    beyond.wait_send()

    @pl.when(worker)
    def _():
        sent(3, 0).wait_send()
        sent(4, 0).wait_send()
        returned(0).wait_send()
        returned(second).wait_send()
        returned(third).wait_send()


def per_device(axis_sizes, boundary, row_tensor, left_proj, right_proj, leg_parity, bond_charges):
    col_dev, sub_rows, merged = boundary.shape
    n_blk = axis_sizes[1]
    padded = n_blk * sub_rows
    rows = row_tensor.transpose(1, 2, 3, 0, 4).reshape(D * D * D * col_dev, D)
    anywhere = pl.BlockSpec(memory_space=pl.ANY)
    smem = pl.BlockSpec(memory_space=pltpu.SMEM)
    vmem = pl.BlockSpec(memory_space=pltpu.VMEM)
    return pl.pallas_call(
        functools.partial(kernel, axis_sizes),
        out_shape=jax.ShapeDtypeStruct(boundary.shape, BF16),
        in_specs=[anywhere, anywhere, anywhere, vmem, smem, smem],
        out_specs=vmem,
        scratch_shapes=[
            pltpu.VMEM((2, padded, merged), BF16),
            pltpu.VMEM((padded, merged), BF16),
            pltpu.VMEM((sub_rows, merged), BF16),
            pltpu.VMEM((2, padded, merged), BF16),
            pltpu.VMEM((2, 2 * LANES, D * LANES), BF16),
            pltpu.VMEM((2, D * sub_rows, 2 * LANES), BF16),
            pltpu.VMEM((2, D * LANES, 2 * LANES), BF16),
            pltpu.VMEM((3, WIDE, WIDE), BF16),
            pltpu.VMEM((2, WIDE, (sub_rows // SUB) * LANES), BF16),
            pltpu.VMEM((2, D * sub_rows, D * LANES), BF16),
            pltpu.VMEM((n_blk, sub_rows, merged), BF16),
            pltpu.SemaphoreType.DMA((7, n_blk)),
            pltpu.SemaphoreType.DMA((7, n_blk)),
            pltpu.SemaphoreType.DMA((6,)),
            pltpu.SemaphoreType.REGULAR((2,)),
        ],
        compiler_params=pltpu.CompilerParams(collective_id=0, has_side_effects=True, vmem_limit_bytes=VMEM_BYTES),
    )(boundary, left_proj, right_proj, rows, leg_parity.transpose(1, 2, 0), bond_charges.transpose(1, 0))


def solution(mesh):
    axis_sizes = (mesh.shape["col"], mesh.shape["blk"])
    in_specs = (
        P(("grp", "col"), "blk", None),
        P(("grp", "col"), None, None, None, None),
        P(("grp", "col"), "blk", None),
        P(("grp", "col"), "blk", None),
        P("grp", None, None),
        P("grp", None),
    )
    out_specs = P(("grp", "col"), "blk", None)
    return jax.shard_map(
        functools.partial(per_device, axis_sizes), mesh=mesh, in_specs=in_specs, out_specs=out_specs, check_vma=False
    )
```

time: 41.3 us -> 43.2 us (1.046); the launches traced: 40.5 us -> 42.9 us
  local copies, waits for them, and re-layouts: 1.66 us -> 5.85 us
  Pallas kernels: 38.8 us -> 37.1 us
    unnamed x1 -> x13, local copies, waits for them, and re-layouts: 1.66 us -> 5.85 us
    pallas_call x1, Pallas kernels: 38.8 us -> 37.1 us  [per_device(): pl.pallas_call(functools.partial(kernel, axis_sizes), out_shape=jax.Shape...]
where the time goes in v2:
time: 43.2 us; the launch traced here: 42.9 us
  Pallas kernels  37.1 us (86%)
  local copies, waits for them, and re-layouts  5.85 us (14%)
    pallas_call x1, Pallas kernels, per_device(): pl.pallas_call(functools.partial(kernel, axis_sizes), out_shape=jax.Shape...  37.1 us
    unnamed x13, local copies, waits for them, and re-layouts  5.85 us

profile of v2, /device:TPU:34, one launch (start us, length us, event | category | flops | bytes accessed | tf_op | source)
XLA Modules:
  0.0 42.9 jit_solution(10093155261873954928)
XLA Ops:
  0.0 0.0 copy-start.5
  0.0 0.7 %copy-done.5 = s32[128,2]{0,1:T(2,128)S(1)} copy-done((s32[128,2]{0,1:T(2,128)S(1)}, s32[128,2]{0,1:T(2,128)}, u32[]{:S(2)}) %copy-start.5) | copy-done | bytes 1048
  0.7 0.0 copy-start
  0.7 0.9 %copy-done = bf16[4,48,576]{2,1,0:T(8,128)(2,1)S(1)} copy-done((bf16[4,48,576]{2,1,0:T(8,128)(2,1)S(1)}, bf16[4,48,576]{2,1,0:T(8,128)(2,1)}, u32[]{:S(2)}) %copy-start) | copy-done | bytes 221208
  1.6 0.0 copy-start.1
  1.6 0.9 %copy-done.1 = bf16[4,48,576]{2,1,0:T(8,128)(2,1)S(1)} copy-done((bf16[4,48,576]{2,1,0:T(8,128)(2,1)S(1)}, bf16[4,48,576]{2,1,0:T(8,128)(2,1)}, u32[]{:S(2)}) %copy-start.1) | copy-done | bytes 221208
  2.6 0.0 copy-start.2
  2.6 0.9 %copy-done.2 = bf16[4,48,576]{2,1,0:T(8,128)(2,1)S(1)} copy-done((bf16[4,48,576]{2,1,0:T(8,128)(2,1)S(1)}, bf16[4,48,576]{2,1,0:T(8,128)(2,1)}, u32[]{:S(2)}) %copy-start.2) | copy-done | bytes 221208
  3.5 0.0 copy-start.3
  3.5 0.9 %copy-done.3 = bf16[4,6,6,6,6]{4,0,3,2,1:T(4,128)(2,1)S(1)} copy-done((bf16[4,6,6,6,6]{4,0,3,2,1:T(4,128)(2,1)S(1)}, bf16[4,6,6,6,6]{4,0,3,2,1:T(4,128)(2,1)}, u32[]{:S(2)}) %copy-start.3) | copy-done | bytes 10392
  4.5 0.0 copy-start.4
  4.5 0.7 %copy-done.4 = s32[128,3,6]{0,2,1:T(8,128)S(1)} copy-done((s32[128,3,6]{0,2,1:T(8,128)S(1)}, s32[128,3,6]{0,2,1:T(8,128)}, u32[]{:S(2)}) %copy-start.4) | copy-done | bytes 9240
  5.2 37.1 %shard_map.64 = bf16[4,48,576]{2,1,0:T(8,128)(2,1)S(1)} custom-call(bf16[4,48,576]{2,1,0:T(8,128)(2,1)S(1)} %copy-done, bf16[4,48,576]{2,1,0:T(8,128)(2,1)S(1)} %copy-done.1, bf16[4,48,576]{2,1,0:T(8,128)(2,1)S(1)} %copy-done.2, bf16[864,6]{1,0:T(8,128)(2,1)S(1)} %bitcast.5, s32[3,6,128]{2,1,0:T(8,128)S(1)} %bitcast.6, s32[2,128]{1,0:T(2,128)S(1)} %bitcast.7), custom_call_target="tpu_custom_call" | custom-call | tf_op jit(solution)/shard_map/pallas_call | solution.py:340
  42.2 0.7 %copy.8 = bf16[4,48,576]{2,1,0:T(8,128)(2,1)} copy(bf16[4,48,576]{2,1,0:T(8,128)(2,1)S(1)} %shard_map.64) | data formatting | bytes 442368
Async XLA Ops:
  0.0 0.7 %copy-start.5 = (s32[128,2]{0,1:T(2,128)S(1)}, s32[128,2]{0,1:T(2,128)}, u32[]{:S(2)}) copy-start(s32[128,2]{0,1:T(2,128)} %param.11) | copy-start | bytes 3076
  0.7 0.9 %copy-start = (bf16[4,48,576]{2,1,0:T(8,128)(2,1)S(1)}, bf16[4,48,576]{2,1,0:T(8,128)(2,1)}, u32[]{:S(2)}) copy-start(bf16[4,48,576]{2,1,0:T(8,128)(2,1)} %bound_ref.1) | copy-start | bytes 663556
  1.6 0.9 %copy-start.1 = (bf16[4,48,576]{2,1,0:T(8,128)(2,1)S(1)}, bf16[4,48,576]{2,1,0:T(8,128)(2,1)}, u32[]{:S(2)}) copy-start(bf16[4,48,576]{2,1,0:T(8,128)(2,1)} %left_ref.1) | copy-start | bytes 663556
  2.6 0.9 %copy-start.2 = (bf16[4,48,576]{2,1,0:T(8,128)(2,1)S(1)}, bf16[4,48,576]{2,1,0:T(8,128)(2,1)}, u32[]{:S(2)}) copy-start(bf16[4,48,576]{2,1,0:T(8,128)(2,1)} %right_ref.1) | copy-start | bytes 663556
  3.5 0.9 %copy-start.3 = (bf16[4,6,6,6,6]{4,0,3,2,1:T(4,128)(2,1)S(1)}, bf16[4,6,6,6,6]{4,0,3,2,1:T(4,128)(2,1)}, u32[]{:S(2)}) copy-start(bf16[4,6,6,6,6]{4,0,3,2,1:T(4,128)(2,1)} %param.7) | copy-start | bytes 31108
  4.5 0.7 %copy-start.4 = (s32[128,3,6]{0,2,1:T(8,128)S(1)}, s32[128,3,6]{0,2,1:T(8,128)}, u32[]{:S(2)}) copy-start(s32[128,3,6]{0,2,1:T(8,128)} %param.10) | copy-start | bytes 27652

commit v3 on v2

--- a/solution.py
+++ b/solution.py
@@ -14,7 +14,7 @@
 SUB = 16
 PAIRS = D * D
 WIDE = PAIRS * SUB
-VMEM_BYTES = 32 * 1024 * 1024
+VMEM_BYTES = 55 * 1024 * 1024
 
 MESH = pl.DeviceIdType.MESH
 F32 = jnp.float32
@@ -40,8 +40,8 @@
     return jnp.where(parity == 0, count, CHI - count)
 
 
-def kernel(axis_sizes, bound_ref, left_ref, right_ref, row_ref, leg_ref, bond_ref, out_ref,
-           bound_all, left_all, left_shared, right_all, bound_x, left_x, right_x, mix, mid, dense, answer,
+def kernel(axis_sizes, bound_ref, left_ref, right_ref, row_hbm, leg_hbm, bond_hbm, out_ref,
+           row_ref, leg_ref, bond_ref, bound_all, left_all, left_shared, right_all, bound_x, left_x, right_x, mix, mid, dense, answer,
            send_sem, recv_sem, local_sem, ready_sem):
     n_col, n_blk = axis_sizes
     col_dev, sub_rows, merged = bound_ref.shape
@@ -50,7 +50,7 @@
     last = n_blk - 1
     col_before = lax.rem(col + n_col - 1, n_col)
     col_after = lax.rem(col + 1, n_col)
-    cols = bond_ref.shape[1]
+    cols = bond_hbm.shape[1]
     worker = me != 0
 
     barrier = pltpu.get_barrier_semaphore()
@@ -74,6 +74,10 @@
     def own(kind):
         return pltpu.make_async_copy(source(kind, me), targets[kind].at[rows(me)], local_sem.at[kind])
 
+    small = [pltpu.make_async_copy(a, b, local_sem.at[6 + i])
+             for i, (a, b) in enumerate([(row_hbm, row_ref), (leg_hbm, leg_ref), (bond_hbm, bond_ref)])]
+    for copy in small:
+        copy.start()
     own(3).start()
     own(4).start()
     own_shared = pltpu.make_async_copy(left_ref.at[0], left_shared, local_sem.at[5])
@@ -124,6 +128,9 @@
                 @pl.when(me != t)
                 def _():
                     sent(kinds_to[t][place], t).start()
+
+    for copy in small:
+        copy.wait()
 
     triples = D * D * D
     group = iota((WIDE, triples), 0) // SUB
@@ -184,25 +191,32 @@
         sent(3, 0).start()
         sent(4, 0).start()
 
+    def pass_beyond():
+        pl.semaphore_wait(ready_sem.at[1], 1)
+        beyond.start()
+
+    @pl.when(col != 0)
+    def _():
+        pass_beyond()
+
     def widened(value, i):
         return jnp.concatenate([value[:, i * BLOCK:(i + 1) * BLOCK], lane_pad], axis=1)
 
-    def all_here(kind):
+    def here(kind, t):
+        @pl.when(me != t)
+        def _():
+            arrived(kind, t).wait_recv()
+
+        @pl.when(me == t)
+        def _():
+            if kind == 2 and t == last:
+                arrived(kind, t).wait_recv()
+            else:
+                own(kind).wait()
+
+    def boundary_ready(slot, bonds):
         for t in reversed(range(n_blk)):
-            @pl.when(me != t)
-            def _():
-                arrived(kind, t).wait_recv()
-
-            @pl.when(me == t)
-            def _():
-                if kind == 2 and t == last:
-                    arrived(kind, t).wait_recv()
-                else:
-                    own(kind).wait()
-
-    def boundary_ready(slot, bonds):
-        all_here(0 if slot else 3)
-        for t in range(n_blk):
+            here(0 if slot else 3, t)
             p, half = t // 2, t % 2
             live = ones_where(half * sub_rows + iota((sub_rows, LANES), 0) < limit_of(bonds[0], p)).astype(BF16)
             value = bound_all[slot, t * sub_rows:(t + 1) * sub_rows, :]
@@ -211,20 +225,23 @@
                 bound_x[slot, at:at + sub_rows, u * LANES:(u + 1) * LANES] = widened(value, u) * live
 
     def right_ready(slot, legs, bonds):
-        all_here(2 if slot else 4)
         pr = legs[3]
-        for half in range(2):
-            even = right_all[slot, half * sub_rows:(half + 1) * sub_rows, :]
-            odd = right_all[slot, BLOCK + half * sub_rows:BLOCK + (half + 1) * sub_rows, :]
+        for t in reversed(range(n_blk)):
+            here(2 if slot else 4, t)
+            p, half = t // 2, t % 2
             position = half * sub_rows + iota((sub_rows, LANES), 0)
-            even_live = ones_where(position < limit_of(bonds[2], 0)).astype(BF16)
-            odd_live = ones_where(position < limit_of(bonds[2], 1)).astype(BF16)
+            live = ones_where(position < limit_of(bonds[2], p)).astype(BF16)
+            value = right_all[slot, t * sub_rows:(t + 1) * sub_rows, :]
             for r in range(D):
-                a = widened(even, r) * even_live
-                b = widened(odd, r) * odd_live
+                wide = widened(value, r) * live
                 at = slice(r * LANES + half * sub_rows, r * LANES + (half + 1) * sub_rows)
-                right_x[slot, at, :LANES] = jnp.where(pr[r] == 0, a, b)
-                right_x[slot, at, LANES:] = jnp.where(pr[r] == 0, b, a)
+
+                if p == 1:
+                    right_x[slot, at, :LANES] = wide
+                    right_x[slot, at, LANES:] = wide
+                else:
+                    right_x[slot, at, :LANES] = jnp.where(pr[r] == 0, wide, right_x[slot, at, :LANES])
+                    right_x[slot, at, LANES:] = jnp.where(pr[r] == 0, right_x[slot, at, LANES:], wide)
 
     groups = sub_rows // SUB
 
@@ -278,15 +295,11 @@
 
     @pl.when(worker)
     def _():
-        all_here(1)
+        for t in range(1, n_blk):
+            here(1, t)
         boundary_ready(1, bonds_mine)
         mixed_rows(1, second, legs_mine, left_all[rows(second), :], 0)
 
-    pl.semaphore_wait(ready_sem.at[1], 1)
-    beyond.start()
-
-    @pl.when(worker)
-    def _():
         right_ready(1, legs_mine, bonds_mine)
         new_rows(1, second, legs_mine, bonds_mine, 0, answer.at[second])
         returned(second).start()
@@ -302,11 +315,16 @@
 
     @pl.when(worker)
     def _():
+        here(1, 0)
         mixed_rows(1, 0, legs_mine, left_all[rows(0), :], 1)
         new_rows(1, 0, legs_mine, bonds_mine, 1, answer.at[0])
         returned(0).start()
         mixed_rows(1, me, legs_mine, left_all[rows(me), :], 0)
         new_rows(1, me, legs_mine, bonds_mine, 0, out_ref.at[me])
+
+    @pl.when(col == 0)
+    def _():
+        pass_beyond()
 
     for t in range(1, n_blk):
         @pl.when(me != t)
@@ -333,16 +351,20 @@
     col_dev, sub_rows, merged = boundary.shape
     n_blk = axis_sizes[1]
     padded = n_blk * sub_rows
+    legs = leg_parity.transpose(1, 2, 0)
+    bonds = bond_charges.transpose(1, 0)
     rows = row_tensor.transpose(1, 2, 3, 0, 4).reshape(D * D * D * col_dev, D)
-    anywhere = pl.BlockSpec(memory_space=pl.ANY)
-    smem = pl.BlockSpec(memory_space=pltpu.SMEM)
+    hbm = pl.BlockSpec(memory_space=pltpu.HBM)
     vmem = pl.BlockSpec(memory_space=pltpu.VMEM)
     return pl.pallas_call(
         functools.partial(kernel, axis_sizes),
-        out_shape=jax.ShapeDtypeStruct(boundary.shape, BF16),
-        in_specs=[anywhere, anywhere, anywhere, vmem, smem, smem],
+        out_shape=pltpu.VMEM(boundary.shape, BF16),
+        in_specs=[hbm] * 6,
         out_specs=vmem,
         scratch_shapes=[
+            pltpu.VMEM(rows.shape, BF16),
+            pltpu.SMEM(legs.shape, jnp.int32),
+            pltpu.SMEM(bonds.shape, jnp.int32),
             pltpu.VMEM((2, padded, merged), BF16),
             pltpu.VMEM((padded, merged), BF16),
             pltpu.VMEM((sub_rows, merged), BF16),
@@ -356,11 +378,11 @@
             pltpu.VMEM((n_blk, sub_rows, merged), BF16),
             pltpu.SemaphoreType.DMA((7, n_blk)),
             pltpu.SemaphoreType.DMA((7, n_blk)),
-            pltpu.SemaphoreType.DMA((6,)),
+            pltpu.SemaphoreType.DMA((9,)),
             pltpu.SemaphoreType.REGULAR((2,)),
         ],
         compiler_params=pltpu.CompilerParams(collective_id=0, has_side_effects=True, vmem_limit_bytes=VMEM_BYTES),
-    )(boundary, left_proj, right_proj, rows, leg_parity.transpose(1, 2, 0), bond_charges.transpose(1, 0))
+    )(boundary, left_proj, right_proj, rows, legs, bonds)
 
 
 def solution(mesh):

time: 43.2 us -> 34.2 us (0.79)
  local copies, waits for them, and re-layouts: 5.85 us -> 0.7 us
  Pallas kernels: 37.1 us -> 33.4 us
    unnamed x13 -> x1, local copies, waits for them, and re-layouts: 5.85 us -> 0.7 us
    pallas_call x1, Pallas kernels: 37.1 us -> 33.4 us  [per_device(): pl.pallas_call(functools.partial(kernel, axis_sizes), out_shape=pltpu.VME...]
where the time goes in v3:
time: 34.2 us; the launch traced here: 34.1 us
  Pallas kernels  33.4 us (98%)
  local copies, waits for them, and re-layouts  0.7 us (2%)
    pallas_call x1, Pallas kernels, per_device(): pl.pallas_call(functools.partial(kernel, axis_sizes), out_shape=pltpu.VME...  33.4 us
    unnamed x1, local copies, waits for them, and re-layouts  0.7 us

profile of v3, /device:TPU:34, one launch (start us, length us, event | category | flops | bytes accessed | tf_op | source)
XLA Modules:
  0.0 34.1 jit_solution(16002349807803433871)
XLA Ops:
  0.0 33.4 %shard_map.64 = bf16[4,48,576]{2,1,0:T(8,128)(2,1)S(1)} custom-call(bf16[4,48,576]{2,1,0:T(8,128)(2,1)} %bound_ref.1, bf16[4,48,576]{2,1,0:T(8,128)(2,1)} %left_ref.1, bf16[4,48,576]{2,1,0:T(8,128)(2,1)} %right_ref.1, bf16[864,6]{1,0:T(8,128)(2,1)} %bitcast.5, s32[3,6,128]{2,1,0:T(8,128)} %bitcast.6, s32[2,128]{1,0:T(2,128)} %bitcast.7), custom_call_target="tpu_custom_call" | custom-call | tf_op jit(solution)/shard_map/pallas_call | solution.py:359
  33.4 0.7 %copy.8 = bf16[4,48,576]{2,1,0:T(8,128)(2,1)} copy(bf16[4,48,576]{2,1,0:T(8,128)(2,1)S(1)} %shard_map.64) | data formatting | bytes 442368

commit v4 on v3

--- a/solution.py
+++ b/solution.py
@@ -121,13 +121,23 @@
         for t in range(n_blk):
             pl.semaphore_signal(ready_sem.at[1], inc=1, device_id={"col": col_after, "blk": t}, device_id_type=MESH)
 
-    kinds_to = {t: ([0, 2, 3, 4, 1] if t != last else [0, 3, 4, 1]) for t in range(1, n_blk)}
-    for place in range(5):
-        for t in (2, 1, 3):
-            if place < len(kinds_to[t]):
-                @pl.when(me != t)
-                def _():
-                    sent(kinds_to[t][place], t).start()
+    kinds_to = {t: ([0, 1, 2, 3, 4] if t != last else [0, 1, 3, 4]) for t in range(1, n_blk)}
+
+    @pl.when(me == 0)
+    def _():
+        for kind in (0, 2, 1, 3, 4):
+            for t in (2, 1, 3):
+                if kind in kinds_to[t]:
+                    sent(kind, t).start()
+
+    @pl.when(worker)
+    def _():
+        for kind in (0, 1, 2, 3, 4):
+            for t in (2, 1, 3):
+                if kind in kinds_to[t]:
+                    @pl.when(me != t)
+                    def _():
+                        sent(kind, t).start()
 
     for copy in small:
         copy.wait()
@@ -307,20 +317,20 @@
         new_rows(1, third, legs_mine, bonds_mine, 1, answer.at[third])
         returned(third).start()
 
+    @pl.when(worker)
+    def _():
+        here(1, 0)
+        mixed_rows(1, 0, legs_mine, left_all[rows(0), :], 0)
+        new_rows(1, 0, legs_mine, bonds_mine, 0, answer.at[0])
+        returned(0).start()
+        mixed_rows(1, me, legs_mine, left_all[rows(me), :], 1)
+        new_rows(1, me, legs_mine, bonds_mine, 1, out_ref.at[me])
+
     boundary_ready(0, bonds_shared)
     own_shared.wait()
     mixed_rows(0, me, legs_shared, left_shared[...], 0)
     right_ready(0, legs_shared, bonds_shared)
     new_rows(0, me, legs_shared, bonds_shared, 0, out_ref.at[0])
-
-    @pl.when(worker)
-    def _():
-        here(1, 0)
-        mixed_rows(1, 0, legs_mine, left_all[rows(0), :], 1)
-        new_rows(1, 0, legs_mine, bonds_mine, 1, answer.at[0])
-        returned(0).start()
-        mixed_rows(1, me, legs_mine, left_all[rows(me), :], 0)
-        new_rows(1, me, legs_mine, bonds_mine, 0, out_ref.at[me])
 
     @pl.when(col == 0)
     def _():

time: 34.2 us -> 34.2 us (level)
  no operation moved by 1% of the time
where the time goes in v4:
time: 34.2 us; the launch traced here: 34.1 us
  Pallas kernels  33.4 us (98%)
  local copies, waits for them, and re-layouts  0.7 us (2%)
    pallas_call x1, Pallas kernels, per_device(): pl.pallas_call(functools.partial(kernel, axis_sizes), out_shape=pltpu.VME...  33.4 us
    unnamed x1, local copies, waits for them, and re-layouts  0.7 us

profile of v4, /device:TPU:34, one launch (start us, length us, event | category | flops | bytes accessed | tf_op | source)
XLA Modules:
  0.0 34.1 jit_solution(17785737671709959110)
XLA Ops:
  0.0 33.4 %shard_map.64 = bf16[4,48,576]{2,1,0:T(8,128)(2,1)S(1)} custom-call(bf16[4,48,576]{2,1,0:T(8,128)(2,1)} %bound_ref.1, bf16[4,48,576]{2,1,0:T(8,128)(2,1)} %left_ref.1, bf16[4,48,576]{2,1,0:T(8,128)(2,1)} %right_ref.1, bf16[864,6]{1,0:T(8,128)(2,1)} %bitcast.5, s32[3,6,128]{2,1,0:T(8,128)} %bitcast.6, s32[2,128]{1,0:T(2,128)} %bitcast.7), custom_call_target="tpu_custom_call" | custom-call | tf_op jit(solution)/shard_map/pallas_call | solution.py:369
  33.4 0.7 %copy.8 = bf16[4,48,576]{2,1,0:T(8,128)(2,1)} copy(bf16[4,48,576]{2,1,0:T(8,128)(2,1)S(1)} %shard_map.64) | data formatting | bytes 442368

commit v5 on v4

--- a/solution.py
+++ b/solution.py
@@ -121,23 +121,34 @@
         for t in range(n_blk):
             pl.semaphore_signal(ready_sem.at[1], inc=1, device_id={"col": col_after, "blk": t}, device_id_type=MESH)
 
+    far = n_blk // 2
     kinds_to = {t: ([0, 1, 2, 3, 4] if t != last else [0, 1, 3, 4]) for t in range(1, n_blk)}
+    kinds_zero = {t: [0, 2, 1, 3, 4] for t in range(1, n_blk)}
+    kinds_zero[far] = [0, 2, 1]
+    kinds_zero[last] = [0, 3, 4, 1]
+    order = [far] + [t for t in range(1, n_blk) if t != far]
 
     @pl.when(me == 0)
     def _():
-        for kind in (0, 2, 1, 3, 4):
-            for t in (2, 1, 3):
-                if kind in kinds_to[t]:
-                    sent(kind, t).start()
-
-    @pl.when(worker)
-    def _():
-        for kind in (0, 1, 2, 3, 4):
-            for t in (2, 1, 3):
+        for place in range(5):
+            for t in order:
+                if place < len(kinds_zero[t]):
+                    sent(kinds_zero[t][place], t).start()
+
+    @pl.when(worker)
+    def _():
+        for kind in range(5):
+            for t in order:
                 if kind in kinds_to[t]:
                     @pl.when(me != t)
                     def _():
                         sent(kind, t).start()
+
+    def passed_on(kind):
+        return pltpu.make_async_remote_copy(
+            src_ref=targets[kind].at[rows(0)], dst_ref=targets[kind].at[rows(0)],
+            send_sem=send_sem.at[6, kind - 2], recv_sem=recv_sem.at[kind, 0],
+            device_id={"blk": far}, device_id_type=MESH)
 
     for copy in small:
         copy.wait()
@@ -161,7 +172,7 @@
         legs = [[leg_ref[i, j, here] for j in range(D)] for i in range(3)] + [[leg_ref[0, j, after] for j in range(D)]]
         return legs, (bond_ref[0, here], bond_ref[1, here], bond_ref[0, after], bond_ref[1, after])
 
-    def build(place, legs, outputs):
+    def build(place, legs, at):
         p0, p1, p2, pr = legs
         pick = ones_where(from_lane == from_row + place).astype(BF16)
         entries = jnp.dot(pick, row_ref[...], preferred_element_type=F32).astype(BF16)
@@ -172,20 +183,19 @@
         legs_r = by_group(pr, lane % D, 1)
         keep = (d_row == lane // D) & ((legs_l + legs_u + legs_d + legs_r) % 2 == 0)
         sign = 1 - 2 * legs_l * legs_u
-        for p, at in outputs:
-            q = (p + legs_d + legs_r) % 2
-            signed = jnp.where(keep, sign * (1 - 2 * q * legs_d), 0).astype(F32)
-            stretched = jnp.dot(repeat, (entries * signed).astype(BF16), preferred_element_type=F32).astype(BF16)
-            full = lax.dot_general(pair, stretched, (((1,), (1,)), ((), ())), preferred_element_type=F32)
-            mix[at] = (full * same).astype(BF16)
+        q = (legs_d + legs_r) % 2
+        signed = jnp.where(keep, sign * (1 - 2 * q * legs_d), 0).astype(F32)
+        stretched = jnp.dot(repeat, (entries * signed).astype(BF16), preferred_element_type=F32).astype(BF16)
+        full = lax.dot_general(pair, stretched, (((1,), (1,)), ((), ())), preferred_element_type=F32)
+        mix[at] = (full * same).astype(BF16)
 
     legs_shared, bonds_shared = legs_of(0)
     legs_mine, bonds_mine = legs_of(me)
-    build(0, legs_shared, [(me // 2, 0)])
-
-    @pl.when(worker)
-    def _():
-        build(me, legs_mine, [(0, 1), (1, 2)])
+    build(0, legs_shared, 0)
+
+    @pl.when(worker)
+    def _():
+        build(me, legs_mine, 1)
 
     gap = LANES - BLOCK
     lane_pad = jnp.zeros((sub_rows, gap), BF16)
@@ -213,7 +223,9 @@
         return jnp.concatenate([value[:, i * BLOCK:(i + 1) * BLOCK], lane_pad], axis=1)
 
     def here(kind, t):
-        @pl.when(me != t)
+        early = t == 0 and kind >= 3
+
+        @pl.when((me != t) & (me != last) if early else me != t)
         def _():
             arrived(kind, t).wait_recv()
 
@@ -255,44 +267,49 @@
 
     groups = sub_rows // SUB
 
-    def mixed_rows(slot, t, legs, value, buf):
-        p = t // 2
-        for leg in range(D):
-            wide = widened(value, leg)
-            odd = ((p + legs[0][leg]) % 2).astype(F32)
-            left_x[buf, leg * sub_rows:(leg + 1) * sub_rows, :LANES] = wide * (1.0 - odd).astype(BF16)
-            left_x[buf, leg * sub_rows:(leg + 1) * sub_rows, LANES:] = wide * odd.astype(BF16)
+    def mixed_rows(slot, units, legs, buf):
+        tall = len(units) * sub_rows
+        for i, (t, value) in enumerate(units):
+            for leg in range(D):
+                wide = widened(value, leg)
+                odd = ((t // 2 + legs[0][leg]) % 2).astype(F32)
+                at = slice(leg * tall + i * sub_rows, leg * tall + (i + 1) * sub_rows)
+                left_x[buf, at, :LANES] = wide * (1.0 - odd).astype(BF16)
+                left_x[buf, at, LANES:] = wide * odd.astype(BF16)
+        count = len(units) * groups
         for n in range(D // 2):
-            part = jnp.dot(left_x[buf], bound_x[slot, :, n * 2 * LANES:(n + 1) * 2 * LANES],
+            part = jnp.dot(left_x[buf, :D * tall], bound_x[slot, :, n * 2 * LANES:(n + 1) * 2 * LANES],
                            preferred_element_type=F32).astype(BF16)
             for leg in range(D):
                 for v in range(2):
                     at = (leg * D + 2 * n + v) * SUB
-                    for g in range(groups):
+                    for g in range(count):
                         mid[buf, at:at + SUB, g * LANES:(g + 1) * LANES] = part[
-                            leg * sub_rows + g * SUB:leg * sub_rows + (g + 1) * SUB, v * LANES:(v + 1) * LANES]
-        which = 0 if slot == 0 else 1 + p
-        for lo in range(0, groups, 2):
-            hi = min(lo + 2, groups)
-            part = jnp.dot(mix[which], mid[buf, :, lo * LANES:hi * LANES], preferred_element_type=F32).astype(BF16)
+                            leg * tall + g * SUB:leg * tall + (g + 1) * SUB, v * LANES:(v + 1) * LANES]
+        for lo in range(0, count, 2):
+            hi = min(lo + 2, count)
+            part = jnp.dot(mix[slot], mid[buf, :, lo * LANES:hi * LANES], preferred_element_type=F32).astype(BF16)
             for d in range(D):
                 for r in range(D):
                     at = (d * D + r) * SUB
                     for g in range(lo, hi):
-                        dense[buf, d * sub_rows + g * SUB:d * sub_rows + (g + 1) * SUB, r * LANES:(r + 1) * LANES] = part[
+                        dense[buf, d * tall + g * SUB:d * tall + (g + 1) * SUB, r * LANES:(r + 1) * LANES] = part[
                             at:at + SUB, (g - lo) * LANES:(g - lo + 1) * LANES]
 
-    def new_rows(slot, t, legs, bonds, buf, target):
-        p = t // 2
-        position = (t % 2) * sub_rows + iota((sub_rows, LANES), 0)
-        row_live = position < limit_of(bonds[1], p)
-        result = jnp.dot(dense[buf], right_x[slot], preferred_element_type=F32)
-        for d in range(D):
-            s = (p + legs[2][d]) % 2
-            block = result[d * sub_rows:(d + 1) * sub_rows, :]
-            chosen = jnp.where(s == 0, block[:, :LANES], block[:, LANES:])
-            alive = row_live & (iota((sub_rows, LANES), 1) < limit_of(bonds[3], s))
-            target[:, d * BLOCK:(d + 1) * BLOCK] = jnp.where(alive, chosen, 0.0).astype(BF16)[:, :BLOCK]
+    def new_rows(slot, units, legs, bonds, buf):
+        tall = len(units) * sub_rows
+        result = jnp.dot(dense[buf, :D * tall], right_x[slot], preferred_element_type=F32)
+        for i, (t, target) in enumerate(units):
+            p = t // 2
+            position = (t % 2) * sub_rows + iota((sub_rows, LANES), 0)
+            row_live = position < limit_of(bonds[1], p)
+            for d in range(D):
+                s = (p + legs[2][d]) % 2
+                at = d * tall + i * sub_rows
+                block = result[at:at + sub_rows, :]
+                chosen = jnp.where(s == 0, block[:, :LANES], block[:, LANES:]) * (1 - 2 * p * legs[2][d]).astype(F32)
+                alive = row_live & (iota((sub_rows, LANES), 1) < limit_of(bonds[3], s))
+                target[:, d * BLOCK:(d + 1) * BLOCK] = jnp.where(alive, chosen, 0.0).astype(BF16)[:, :BLOCK]
 
     def returned(t):
         return pltpu.make_async_remote_copy(
@@ -308,29 +325,30 @@
         for t in range(1, n_blk):
             here(1, t)
         boundary_ready(1, bonds_mine)
-        mixed_rows(1, second, legs_mine, left_all[rows(second), :], 0)
-
+        mixed_rows(1, [(t, left_all[rows(t), :]) for t in (second, third)], legs_mine, 0)
+
+    @pl.when(me == last)
+    def _():
+        for kind in (3, 4):
+            arrived(kind, 0).wait_recv()
+            passed_on(kind).start()
+
+    @pl.when(worker)
+    def _():
         right_ready(1, legs_mine, bonds_mine)
-        new_rows(1, second, legs_mine, bonds_mine, 0, answer.at[second])
+        new_rows(1, [(t, answer.at[t]) for t in (second, third)], legs_mine, bonds_mine, 0)
         returned(second).start()
-        mixed_rows(1, third, legs_mine, left_all[rows(third), :], 1)
-        new_rows(1, third, legs_mine, bonds_mine, 1, answer.at[third])
         returned(third).start()
-
-    @pl.when(worker)
-    def _():
         here(1, 0)
-        mixed_rows(1, 0, legs_mine, left_all[rows(0), :], 0)
-        new_rows(1, 0, legs_mine, bonds_mine, 0, answer.at[0])
+        mixed_rows(1, [(0, left_all[rows(0), :]), (me, left_all[rows(me), :])], legs_mine, 1)
+        new_rows(1, [(0, answer.at[0]), (me, out_ref.at[me])], legs_mine, bonds_mine, 1)
         returned(0).start()
-        mixed_rows(1, me, legs_mine, left_all[rows(me), :], 1)
-        new_rows(1, me, legs_mine, bonds_mine, 1, out_ref.at[me])
 
     boundary_ready(0, bonds_shared)
     own_shared.wait()
-    mixed_rows(0, me, legs_shared, left_shared[...], 0)
+    mixed_rows(0, [(me, left_shared[...])], legs_shared, 0)
     right_ready(0, legs_shared, bonds_shared)
-    new_rows(0, me, legs_shared, bonds_shared, 0, out_ref.at[0])
+    new_rows(0, [(me, out_ref.at[0])], legs_shared, bonds_shared, 0)
 
     @pl.when(col == 0)
     def _():
@@ -343,13 +361,28 @@
                 src_ref=answer.at[t], dst_ref=out_ref.at[t],
                 send_sem=send_sem.at[5, t], recv_sem=recv_sem.at[5, t],
                 device_id={"blk": t}, device_id_type=MESH).wait_recv()
-            for kind in kinds_to[t]:
+
+    @pl.when(me == 0)
+    def _():
+        for t in order:
+            for kind in kinds_zero[t]:
                 sent(kind, t).wait_send()
 
+    @pl.when(me == last)
+    def _():
+        passed_on(3).wait_send()
+        passed_on(4).wait_send()
+
     beyond.wait_send()
 
     @pl.when(worker)
     def _():
+        for t in order:
+            @pl.when(me != t)
+            def _():
+                for kind in kinds_to[t]:
+                    sent(kind, t).wait_send()
+
         sent(3, 0).wait_send()
         sent(4, 0).wait_send()
         returned(0).wait_send()
@@ -380,11 +413,11 @@
             pltpu.VMEM((sub_rows, merged), BF16),
             pltpu.VMEM((2, padded, merged), BF16),
             pltpu.VMEM((2, 2 * LANES, D * LANES), BF16),
-            pltpu.VMEM((2, D * sub_rows, 2 * LANES), BF16),
+            pltpu.VMEM((2, 2 * D * sub_rows, 2 * LANES), BF16),
             pltpu.VMEM((2, D * LANES, 2 * LANES), BF16),
-            pltpu.VMEM((3, WIDE, WIDE), BF16),
-            pltpu.VMEM((2, WIDE, (sub_rows // SUB) * LANES), BF16),
-            pltpu.VMEM((2, D * sub_rows, D * LANES), BF16),
+            pltpu.VMEM((2, WIDE, WIDE), BF16),
+            pltpu.VMEM((2, WIDE, 2 * (sub_rows // SUB) * LANES), BF16),
+            pltpu.VMEM((2, 2 * D * sub_rows, D * LANES), BF16),
             pltpu.VMEM((n_blk, sub_rows, merged), BF16),
             pltpu.SemaphoreType.DMA((7, n_blk)),
             pltpu.SemaphoreType.DMA((7, n_blk)),

time: 34.2 us -> 33.1 us (0.968)
  Pallas kernels: 33.4 us -> 32.3 us
    pallas_call x1, Pallas kernels: 33.4 us -> 32.3 us  [per_device(): pl.pallas_call(functools.partial(kernel, axis_sizes), out_shape=pltpu.VME...]
where the time goes in v5:
time: 33.1 us; the launch traced here: 33 us
  Pallas kernels  32.3 us (98%)
  local copies, waits for them, and re-layouts  0.7 us (2%)
    pallas_call x1, Pallas kernels, per_device(): pl.pallas_call(functools.partial(kernel, axis_sizes), out_shape=pltpu.VME...  32.3 us
    unnamed x1, local copies, waits for them, and re-layouts  0.7 us

profile of v5, /device:TPU:34, one launch (start us, length us, event | category | flops | bytes accessed | tf_op | source)
XLA Modules:
  0.0 33.0 jit_solution(18202950046917164492)
XLA Ops:
  0.0 32.3 %shard_map.64 = bf16[4,48,576]{2,1,0:T(8,128)(2,1)S(1)} custom-call(bf16[4,48,576]{2,1,0:T(8,128)(2,1)} %bound_ref.1, bf16[4,48,576]{2,1,0:T(8,128)(2,1)} %left_ref.1, bf16[4,48,576]{2,1,0:T(8,128)(2,1)} %right_ref.1, bf16[864,6]{1,0:T(8,128)(2,1)} %bitcast.5, s32[3,6,128]{2,1,0:T(8,128)} %bitcast.6, s32[2,128]{1,0:T(2,128)} %bitcast.7), custom_call_target="tpu_custom_call" | custom-call | tf_op jit(solution)/shard_map/pallas_call | solution.py:402
  32.3 0.7 %copy.8 = bf16[4,48,576]{2,1,0:T(8,128)(2,1)} copy(bf16[4,48,576]{2,1,0:T(8,128)(2,1)S(1)} %shard_map.64) | data formatting | bytes 442368

commit v6 on v5

--- a/solution.py
+++ b/solution.py
@@ -41,7 +41,7 @@
 
 
 def kernel(axis_sizes, bound_ref, left_ref, right_ref, row_hbm, leg_hbm, bond_hbm, out_ref,
-           row_ref, leg_ref, bond_ref, bound_all, left_all, left_shared, right_all, bound_x, left_x, right_x, mix, mid, dense, answer,
+           row_ref, leg_ref, bond_ref, bond_rows, bound_all, left_all, left_shared, right_all, bound_x, left_x, right_x, mix, mid, dense, answer,
            send_sem, recv_sem, local_sem, ready_sem):
     n_col, n_blk = axis_sizes
     col_dev, sub_rows, merged = bound_ref.shape
@@ -75,7 +75,7 @@
         return pltpu.make_async_copy(source(kind, me), targets[kind].at[rows(me)], local_sem.at[kind])
 
     small = [pltpu.make_async_copy(a, b, local_sem.at[6 + i])
-             for i, (a, b) in enumerate([(row_hbm, row_ref), (leg_hbm, leg_ref), (bond_hbm, bond_ref)])]
+             for i, (a, b) in enumerate([(row_hbm, row_ref), (leg_hbm, leg_ref), (bond_hbm, bond_ref), (right_ref.at[0], bond_rows)])]
     for copy in small:
         copy.start()
     own(3).start()
@@ -107,7 +107,7 @@
             device_id={"blk": t}, device_id_type=MESH)
 
     beyond = pltpu.make_async_remote_copy(
-        src_ref=right_ref.at[0], dst_ref=right_all.at[1, rows(me)],
+        src_ref=bond_rows, dst_ref=right_all.at[1, rows(me)],
         send_sem=send_sem.at[6, 0], recv_sem=recv_sem.at[2, me],
         device_id={"col": col_before, "blk": last}, device_id_type=MESH)
 
@@ -339,20 +339,28 @@
         new_rows(1, [(t, answer.at[t]) for t in (second, third)], legs_mine, bonds_mine, 0)
         returned(second).start()
         returned(third).start()
+
+    @pl.when(worker)
+    def _():
         here(1, 0)
-        mixed_rows(1, [(0, left_all[rows(0), :]), (me, left_all[rows(me), :])], legs_mine, 1)
-        new_rows(1, [(0, answer.at[0]), (me, out_ref.at[me])], legs_mine, bonds_mine, 1)
+        mixed_rows(1, [(0, left_all[rows(0), :])], legs_mine, 1)
+        new_rows(1, [(0, answer.at[0])], legs_mine, bonds_mine, 1)
         returned(0).start()
+
+    @pl.when(col == 0)
+    def _():
+        pass_beyond()
+
+    @pl.when(worker)
+    def _():
+        mixed_rows(1, [(me, left_all[rows(me), :])], legs_mine, 0)
+        new_rows(1, [(me, out_ref.at[me])], legs_mine, bonds_mine, 0)
 
     boundary_ready(0, bonds_shared)
     own_shared.wait()
-    mixed_rows(0, [(me, left_shared[...])], legs_shared, 0)
+    mixed_rows(0, [(me, left_shared[...])], legs_shared, 1)
     right_ready(0, legs_shared, bonds_shared)
-    new_rows(0, [(me, out_ref.at[0])], legs_shared, bonds_shared, 0)
-
-    @pl.when(col == 0)
-    def _():
-        pass_beyond()
+    new_rows(0, [(me, out_ref.at[0])], legs_shared, bonds_shared, 1)
 
     for t in range(1, n_blk):
         @pl.when(me != t)
@@ -408,6 +416,7 @@
             pltpu.VMEM(rows.shape, BF16),
             pltpu.SMEM(legs.shape, jnp.int32),
             pltpu.SMEM(bonds.shape, jnp.int32),
+            pltpu.VMEM((sub_rows, merged), BF16),
             pltpu.VMEM((2, padded, merged), BF16),
             pltpu.VMEM((padded, merged), BF16),
             pltpu.VMEM((sub_rows, merged), BF16),
@@ -421,7 +430,7 @@
             pltpu.VMEM((n_blk, sub_rows, merged), BF16),
             pltpu.SemaphoreType.DMA((7, n_blk)),
             pltpu.SemaphoreType.DMA((7, n_blk)),
-            pltpu.SemaphoreType.DMA((9,)),
+            pltpu.SemaphoreType.DMA((10,)),
             pltpu.SemaphoreType.REGULAR((2,)),
         ],
         compiler_params=pltpu.CompilerParams(collective_id=0, has_side_effects=True, vmem_limit_bytes=VMEM_BYTES),

time: 33.1 us -> 31.6 us (0.955)
  Pallas kernels: 32.3 us -> 30.8 us
    pallas_call x1, Pallas kernels: 32.3 us -> 30.8 us  [per_device(): pl.pallas_call(functools.partial(kernel, axis_sizes), out_shape=pltpu.VME...]
where the time goes in v6:
time: 31.6 us; the launch traced here: 31.5 us
  Pallas kernels  30.8 us (97%)
  local copies, waits for them, and re-layouts  0.7 us (2%)
    pallas_call x1, Pallas kernels, per_device(): pl.pallas_call(functools.partial(kernel, axis_sizes), out_shape=pltpu.VME...  30.8 us
    unnamed x1, local copies, waits for them, and re-layouts  0.7 us

profile of v6, /device:TPU:34, one launch (start us, length us, event | category | flops | bytes accessed | tf_op | source)
XLA Modules:
  0.0 31.5 jit_solution(17270801644056313033)
XLA Ops:
  0.0 30.8 %shard_map.64 = bf16[4,48,576]{2,1,0:T(8,128)(2,1)S(1)} custom-call(bf16[4,48,576]{2,1,0:T(8,128)(2,1)} %bound_ref.1, bf16[4,48,576]{2,1,0:T(8,128)(2,1)} %left_ref.1, bf16[4,48,576]{2,1,0:T(8,128)(2,1)} %right_ref.1, bf16[864,6]{1,0:T(8,128)(2,1)} %bitcast.5, s32[3,6,128]{2,1,0:T(8,128)} %bitcast.6, s32[2,128]{1,0:T(2,128)} %bitcast.7), custom_call_target="tpu_custom_call" | custom-call | tf_op jit(solution)/shard_map/pallas_call | solution.py:410
  30.8 0.7 %copy.8 = bf16[4,48,576]{2,1,0:T(8,128)(2,1)} copy(bf16[4,48,576]{2,1,0:T(8,128)(2,1)S(1)} %shard_map.64) | data formatting | bytes 442368

commit v7 on v6

--- a/solution.py
+++ b/solution.py
@@ -76,15 +76,18 @@
 
     small = [pltpu.make_async_copy(a, b, local_sem.at[6 + i])
              for i, (a, b) in enumerate([(row_hbm, row_ref), (leg_hbm, leg_ref), (bond_hbm, bond_ref), (right_ref.at[0], bond_rows)])]
-    for copy in small:
-        copy.start()
-    own(3).start()
-    own(4).start()
     own_shared = pltpu.make_async_copy(left_ref.at[0], left_shared, local_sem.at[5])
-    own_shared.start()
-
-    @pl.when(worker)
-    def _():
+
+    def fetch():
+        for copy in small:
+            copy.start()
+        own(3).start()
+        own(4).start()
+        own_shared.start()
+
+    @pl.when(worker)
+    def _():
+        fetch()
         own(0).start()
         own(1).start()
 
@@ -134,6 +137,7 @@
             for t in order:
                 if place < len(kinds_zero[t]):
                     sent(kinds_zero[t][place], t).start()
+        fetch()
 
     @pl.when(worker)
     def _():
@@ -267,16 +271,19 @@
 
     groups = sub_rows // SUB
 
-    def mixed_rows(slot, units, legs, buf):
-        tall = len(units) * sub_rows
-        for i, (t, value) in enumerate(units):
+    def spread_left(units, legs, buf, first=0, count=None):
+        tall = (count or len(units)) * sub_rows
+        for i, (t, value) in enumerate(units, first):
             for leg in range(D):
                 wide = widened(value, leg)
                 odd = ((t // 2 + legs[0][leg]) % 2).astype(F32)
                 at = slice(leg * tall + i * sub_rows, leg * tall + (i + 1) * sub_rows)
                 left_x[buf, at, :LANES] = wide * (1.0 - odd).astype(BF16)
                 left_x[buf, at, LANES:] = wide * odd.astype(BF16)
-        count = len(units) * groups
+
+    def mixed_rows(slot, units, buf):
+        tall = units * sub_rows
+        count = units * groups
         for n in range(D // 2):
             part = jnp.dot(left_x[buf, :D * tall], bound_x[slot, :, n * 2 * LANES:(n + 1) * 2 * LANES],
                            preferred_element_type=F32).astype(BF16)
@@ -320,12 +327,22 @@
     second = 1 + lax.rem(me, last)
     third = 1 + lax.rem(second, last)
 
+    def pass_beyond_first():
+        @pl.when(col == 0)
+        def _():
+            pass_beyond()
+
+    own_shared.wait()
+    spread_left([(me, left_shared[...])], legs_shared, 2)
+
     @pl.when(worker)
     def _():
         for t in range(1, n_blk):
             here(1, t)
+        spread_left([(t, left_all[rows(t), :]) for t in (second, third)], legs_mine, 0)
+        spread_left([(me, left_all[rows(me), :])], legs_mine, 1, 1, 2)
         boundary_ready(1, bonds_mine)
-        mixed_rows(1, [(t, left_all[rows(t), :]) for t in (second, third)], legs_mine, 0)
+        mixed_rows(1, 2, 0)
 
     @pl.when(me == last)
     def _():
@@ -343,24 +360,20 @@
     @pl.when(worker)
     def _():
         here(1, 0)
-        mixed_rows(1, [(0, left_all[rows(0), :])], legs_mine, 1)
-        new_rows(1, [(0, answer.at[0])], legs_mine, bonds_mine, 1)
+        spread_left([(0, left_all[rows(0), :])], legs_mine, 1, 0, 2)
+        mixed_rows(1, 2, 1)
+        new_rows(1, [(0, answer.at[0]), (me, out_ref.at[me])], legs_mine, bonds_mine, 1)
         returned(0).start()
-
-    @pl.when(col == 0)
-    def _():
-        pass_beyond()
-
-    @pl.when(worker)
-    def _():
-        mixed_rows(1, [(me, left_all[rows(me), :])], legs_mine, 0)
-        new_rows(1, [(me, out_ref.at[me])], legs_mine, bonds_mine, 0)
+        pass_beyond_first()
+
+    @pl.when(me == 0)
+    def _():
+        pass_beyond_first()
 
     boundary_ready(0, bonds_shared)
-    own_shared.wait()
-    mixed_rows(0, [(me, left_shared[...])], legs_shared, 1)
+    mixed_rows(0, 1, 2)
     right_ready(0, legs_shared, bonds_shared)
-    new_rows(0, [(me, out_ref.at[0])], legs_shared, bonds_shared, 1)
+    new_rows(0, [(me, out_ref.at[0])], legs_shared, bonds_shared, 2)
 
     for t in range(1, n_blk):
         @pl.when(me != t)
@@ -422,11 +435,11 @@
             pltpu.VMEM((sub_rows, merged), BF16),
             pltpu.VMEM((2, padded, merged), BF16),
             pltpu.VMEM((2, 2 * LANES, D * LANES), BF16),
-            pltpu.VMEM((2, 2 * D * sub_rows, 2 * LANES), BF16),
+            pltpu.VMEM((3, 2 * D * sub_rows, 2 * LANES), BF16),
             pltpu.VMEM((2, D * LANES, 2 * LANES), BF16),
             pltpu.VMEM((2, WIDE, WIDE), BF16),
-            pltpu.VMEM((2, WIDE, 2 * (sub_rows // SUB) * LANES), BF16),
-            pltpu.VMEM((2, 2 * D * sub_rows, D * LANES), BF16),
+            pltpu.VMEM((3, WIDE, 2 * (sub_rows // SUB) * LANES), BF16),
+            pltpu.VMEM((3, 2 * D * sub_rows, D * LANES), BF16),
             pltpu.VMEM((n_blk, sub_rows, merged), BF16),
             pltpu.SemaphoreType.DMA((7, n_blk)),
             pltpu.SemaphoreType.DMA((7, n_blk)),

time: 31.6 us -> 30.9 us (0.978)
  Pallas kernels: 30.8 us -> 30.1 us
    pallas_call x1, Pallas kernels: 30.8 us -> 30.1 us  [per_device(): pl.pallas_call(functools.partial(kernel, axis_sizes), out_shape=pltpu.VME...]
where the time goes in v7:
time: 30.9 us; the launch traced here: 30.8 us
  Pallas kernels  30.1 us (97%)
  local copies, waits for them, and re-layouts  0.7 us (2%)
    pallas_call x1, Pallas kernels, per_device(): pl.pallas_call(functools.partial(kernel, axis_sizes), out_shape=pltpu.VME...  30.1 us
    unnamed x1, local copies, waits for them, and re-layouts  0.7 us

profile of v7, /device:TPU:34, one launch (start us, length us, event | category | flops | bytes accessed | tf_op | source)
XLA Modules:
  0.0 30.8 jit_solution(9352197320039396809)
XLA Ops:
  0.0 30.1 %shard_map.64 = bf16[4,48,576]{2,1,0:T(8,128)(2,1)S(1)} custom-call(bf16[4,48,576]{2,1,0:T(8,128)(2,1)} %bound_ref.1, bf16[4,48,576]{2,1,0:T(8,128)(2,1)} %left_ref.1, bf16[4,48,576]{2,1,0:T(8,128)(2,1)} %right_ref.1, bf16[864,6]{1,0:T(8,128)(2,1)} %bitcast.5, s32[3,6,128]{2,1,0:T(8,128)} %bitcast.6, s32[2,128]{1,0:T(2,128)} %bitcast.7), custom_call_target="tpu_custom_call" | custom-call | tf_op jit(solution)/shard_map/pallas_call | solution.py:423
  30.1 0.7 %copy.8 = bf16[4,48,576]{2,1,0:T(8,128)(2,1)} copy(bf16[4,48,576]{2,1,0:T(8,128)(2,1)S(1)} %shard_map.64) | data formatting | bytes 442368

commit v8 on v7

--- a/solution.py
+++ b/solution.py
@@ -240,8 +240,8 @@
             else:
                 own(kind).wait()
 
-    def boundary_ready(slot, bonds):
-        for t in reversed(range(n_blk)):
+    def boundary_ready(slot, bonds, places):
+        for t in places:
             here(0 if slot else 3, t)
             p, half = t // 2, t % 2
             live = ones_where(half * sub_rows + iota((sub_rows, LANES), 0) < limit_of(bonds[0], p)).astype(BF16)
@@ -250,9 +250,9 @@
             for u in range(D):
                 bound_x[slot, at:at + sub_rows, u * LANES:(u + 1) * LANES] = widened(value, u) * live
 
-    def right_ready(slot, legs, bonds):
+    def right_ready(slot, legs, bonds, places):
         pr = legs[3]
-        for t in reversed(range(n_blk)):
+        for t in places:
             here(2 if slot else 4, t)
             p, half = t // 2, t % 2
             position = half * sub_rows + iota((sub_rows, LANES), 0)
@@ -324,6 +324,7 @@
             send_sem=send_sem.at[5, t], recv_sem=recv_sem.at[5, me],
             device_id={"blk": t}, device_id_type=MESH)
 
+    everyone = list(reversed(range(n_blk)))
     second = 1 + lax.rem(me, last)
     third = 1 + lax.rem(second, last)
 
@@ -341,7 +342,7 @@
             here(1, t)
         spread_left([(t, left_all[rows(t), :]) for t in (second, third)], legs_mine, 0)
         spread_left([(me, left_all[rows(me), :])], legs_mine, 1, 1, 2)
-        boundary_ready(1, bonds_mine)
+        boundary_ready(1, bonds_mine, everyone)
         mixed_rows(1, 2, 0)
 
     @pl.when(me == last)
@@ -352,10 +353,13 @@
 
     @pl.when(worker)
     def _():
-        right_ready(1, legs_mine, bonds_mine)
+        right_ready(1, legs_mine, bonds_mine, everyone)
         new_rows(1, [(t, answer.at[t]) for t in (second, third)], legs_mine, bonds_mine, 0)
         returned(second).start()
         returned(third).start()
+
+    boundary_ready(0, bonds_shared, everyone[:-1])
+    right_ready(0, legs_shared, bonds_shared, everyone[:-1])
 
     @pl.when(worker)
     def _():
@@ -370,9 +374,9 @@
     def _():
         pass_beyond_first()
 
-    boundary_ready(0, bonds_shared)
+    boundary_ready(0, bonds_shared, everyone[-1:])
     mixed_rows(0, 1, 2)
-    right_ready(0, legs_shared, bonds_shared)
+    right_ready(0, legs_shared, bonds_shared, everyone[-1:])
     new_rows(0, [(me, out_ref.at[0])], legs_shared, bonds_shared, 2)
 
     for t in range(1, n_blk):

time: 30.9 us -> 30.8 us (level)
  no operation moved by 1% of the time
where the time goes in v8:
time: 30.8 us; the launch traced here: 30.7 us
  Pallas kernels  30 us (97%)
  local copies, waits for them, and re-layouts  0.7 us (2%)
    pallas_call x1, Pallas kernels, per_device(): pl.pallas_call(functools.partial(kernel, axis_sizes), out_shape=pltpu.VME...  30 us
    unnamed x1, local copies, waits for them, and re-layouts  0.7 us

profile of v8, /device:TPU:34, one launch (start us, length us, event | category | flops | bytes accessed | tf_op | source)
XLA Modules:
  0.0 30.7 jit_solution(2930174525751748852)
XLA Ops:
  0.0 30.0 %shard_map.64 = bf16[4,48,576]{2,1,0:T(8,128)(2,1)S(1)} custom-call(bf16[4,48,576]{2,1,0:T(8,128)(2,1)} %bound_ref.1, bf16[4,48,576]{2,1,0:T(8,128)(2,1)} %left_ref.1, bf16[4,48,576]{2,1,0:T(8,128)(2,1)} %right_ref.1, bf16[864,6]{1,0:T(8,128)(2,1)} %bitcast.5, s32[3,6,128]{2,1,0:T(8,128)} %bitcast.6, s32[2,128]{1,0:T(2,128)} %bitcast.7), custom_call_target="tpu_custom_call" | custom-call | tf_op jit(solution)/shard_map/pallas_call | solution.py:427
  30.0 0.7 %copy.8 = bf16[4,48,576]{2,1,0:T(8,128)(2,1)} copy(bf16[4,48,576]{2,1,0:T(8,128)(2,1)S(1)} %shard_map.64) | data formatting | bytes 442368
